TPU v7x, 256 devices: a whole 4x4x8 slice. The times are simulated.
256 devices in a mesh: section: 16 (over z, x_hi), tensor: 16 (over x_lo, y, core).
Axes of the slice: x: 4 (x_hi: 2, x_lo: 2; x = x_hi * 2 + x_lo), y: 4, z: 8, core: 2. Of those that a mesh axis runs over, the one named last changes fastest.
Arguments:
- noise: float32 [2, 4, 32, 32], P(None, None, 'tensor'), may hold values from -6 to 6
- target: float32 [2, 4, 32, 32], P(None, None, 'tensor'), may hold values from -6 to 6
- timesteps: int32 [16], replicated, may hold values from 1 to 320, as said below
- w_in: float32 [4, 320], replicated, may hold values from -3 to 3
- gn_gain: float32 [320], replicated, may hold values from 0.1 to 1.9
- w_time1: float32 [320, 1280], replicated, may hold values from -0.3125 to 0.3125
- w_time2: float32 [1280, 320], replicated, may hold values from -0.15625 to 0.15625
- w_conv: bfloat16 [9, 320, 320], replicated, may hold values from -0.109375 to 0.109375
- w_out: float32 [320, 4], replicated, may hold values from -0.3125 to 0.3125
Outputs:
- trajectory: float32 [16, 2, 4, 32, 32], P('section', None, None, 'tensor')
- grad_conv: float32 [9, 320, 320], P(None, None, 'tensor')
Inputs may be any that keep to these rules, and one draw needn't show every extreme that they name: `timesteps`: 16 distinct plan indices, strictly falling from one step to the next.
All inputs are finite; a program needn't handle non-finite values.
Results may differ from a plain program's by a relative error of at most 0.0008.
Values sent between devices are 32-bit elements; how exact they have to be, the bound alone decides.
No kernel may reach another device: no remote copies, remote signals or barrier semaphores. Data moves between devices by JAX's collectives and lax.ppermute only.
A program may use at most 64 MiB of HBM per device.

v0:
```python
import math

import jax
import jax.numpy as jnp
from jax import lax
from jax.sharding import PartitionSpec as P

GROUPS = 32


precise = lax.Precision.HIGHEST


def extended(cells, sides, width):
    for axis, dim in sides:
        count = lax.axis_size(axis)
        ends = count - 1
        head = lax.slice_in_dim(cells, 0, width, axis=dim)
        tail = lax.slice_in_dim(cells, cells.shape[dim] - width, cells.shape[dim], axis=dim)
        cells = jnp.concatenate(
            [
                lax.ppermute(tail, axis, [(i, (i + 1) % count) for i in range(ends)]),
                cells,
                lax.ppermute(head, axis, [((i + 1) % count, i) for i in range(ends)]),
            ],
            axis=dim,
        )
    return cells


def from_everyone(x, axis):
    size = lax.axis_size(axis)
    return lax.all_to_all(jnp.broadcast_to(x[None], (size, *x.shape)), axis, 0, 0, tiled=True)


def over_copies(x, axis):
    return from_everyone(x, axis).sum(axis=0)


def in_one(arrays, axis):
    line, at, done = (jnp.concatenate([a.reshape(-1) for a in arrays]), 0, [])
    total = over_copies(line, axis)
    for a in arrays:
        done.append(total[at : at + a.size].reshape(a.shape))
        at += a.size
    return tuple(done)


def passed_along(block, axis, distance):
    devices = range(lax.axis_size(axis))
    route = [(i - distance, i) for i in devices if i - distance in devices]
    return lax.ppermute(block, axis, route)


def alpha_table():
    step_grid = jnp.arange(1000, dtype=jnp.float32)
    lowest = jnp.sqrt(jnp.asarray(0.00085, jnp.float32))
    highest = jnp.sqrt(jnp.asarray(0.012, jnp.float32))
    betas = (lowest + step_grid * ((highest - lowest) / 999.0)) ** 2
    return jnp.cumprod(1.0 - betas)


def section_terms(timesteps, section_index, alphas, w_time1, w_time2, features):
    positions = jnp.arange(timesteps.shape[0], dtype=jnp.int32)
    current = jnp.sum(jnp.where(positions == section_index, timesteps, 0))
    following = jnp.sum(jnp.where(positions == section_index + 1, timesteps, 0))
    step_grid = jnp.arange(alphas.shape[0], dtype=jnp.int32)
    alpha_now = jnp.sum(jnp.where(step_grid == current, alphas, 0.0))
    alpha_next = jnp.where(
        section_index + 1 < timesteps.shape[0],
        jnp.sum(jnp.where(step_grid == following, alphas, 0.0)),
        1.0,
    )
    keep_coef = jnp.sqrt(alpha_next / alpha_now)
    noise_coef = jnp.sqrt(1.0 - alpha_next) - keep_coef * jnp.sqrt(1.0 - alpha_now)
    half_width = features // 2
    frequency = jnp.exp(-math.log(10000.0) * jnp.arange(half_width, dtype=jnp.float32) / half_width)
    angles = current.astype(jnp.float32) * frequency
    sinusoid = jnp.concatenate([jnp.cos(angles), jnp.sin(angles)])
    hidden = jax.nn.silu(jnp.dot(sinusoid, w_time1, precision=precise))
    return (keep_coef, noise_coef, jnp.dot(hidden, w_time2, precision=precise))


def group_partial(latent, w_in, groups):
    projected = jnp.einsum("crw,cd->rwd", latent, w_in, precision=precise)
    grouped = projected.reshape(-1, groups, projected.shape[2] // groups)
    return (jnp.sum(grouped, axis=(0, 2)), jnp.sum(grouped * grouped, axis=(0, 2)))


def local(noise, target, timesteps, w_in, gn_gain, w_time1, w_time2, w_conv, w_out):
    sections = lax.axis_size("section")
    section_index = lax.axis_index("section")
    tensor_size = lax.axis_size("tensor")
    tensor_index = lax.axis_index("tensor")
    micro_count, channels, row_count, breadth = noise.shape
    features = w_in.shape[1]
    height = row_count * tensor_size
    count_all = jnp.asarray(height * breadth * (features // GROUPS), jnp.float32)
    alphas = alpha_table()
    keep_coef, noise_coef, embed = section_terms(
        timesteps, section_index, alphas, w_time1, w_time2, features
    )
    wide_conv = w_conv.astype(jnp.float32)
    global_rows = tensor_index * row_count - 1 + jnp.arange(row_count + 2, dtype=jnp.int32)
    row_mask = ((global_rows >= 0) & (global_rows < height)).astype(jnp.float32)
    ticks = sections + micro_count - 1

    def exchange_rows(block):
        return extended(block, (("tensor", 1),), 1)

    def total_stats(pair):
        return in_one((pair[0], pair[1]), "tensor")

    def prepare(latent_pad, group_sum, squares):
        projected = jnp.einsum("crw,cd->rwd", latent_pad, w_in, precision=precise)
        group_avg = group_sum / count_all
        group_var = squares / count_all - group_avg * group_avg
        average = jnp.repeat(group_avg, features // GROUPS)
        variance = jnp.repeat(group_var, features // GROUPS)
        activated = (
            jax.nn.silu((projected - average) * lax.rsqrt(variance + 1e-05) * gn_gain)
            * row_mask[:, None, None]
        )
        activated = activated + lax.stop_gradient(
            activated.astype(jnp.bfloat16).astype(jnp.float32) - activated
        )
        return (projected, jnp.pad(activated, ((0, 0), (1, 1), (0, 0))))

    def finish(latent_pad, projected, convolved):
        hidden = projected[1:-1] + convolved + embed
        guess = jnp.einsum("rwd,dc->crw", hidden, w_out, precision=precise)
        return keep_coef * latent_pad[:, 1:-1] + noise_coef * guess

    def step_rows(latent_pad, group_sum, squares):
        projected, activated = prepare(latent_pad, group_sum, squares)
        narrow = activated.astype(jnp.bfloat16)
        convolved = jnp.zeros((row_count, breadth, features), jnp.float32)
        for offset in range(9):
            shift_row = offset // 3
            shift_col = offset % 3
            window = narrow[shift_row : shift_row + row_count, shift_col : shift_col + breadth]
            convolved = convolved + jnp.einsum(
                "rwc,cd->rwd", window, w_conv[offset], preferred_element_type=jnp.float32
            )
        return finish(latent_pad, projected, convolved)

    def forward_tick(tick, carry):
        outgoing, saved_pad, saved_sum, saved_square, path = carry
        arrived = passed_along(outgoing, "section", 1)
        micro_index = tick - section_index
        active = (micro_index >= 0) & (micro_index < micro_count)
        slot = jnp.clip(micro_index, 0, micro_count - 1)
        starting = lax.dynamic_index_in_dim(noise, slot, 0, keepdims=False)
        latent = jnp.where(section_index == 0, starting, arrived)
        latent_pad = exchange_rows(latent)
        group_sum, squares = total_stats(group_partial(latent, w_in, GROUPS))
        stepped = lax.cond(
            active,
            lambda: step_rows(latent_pad, group_sum, squares),
            lambda: jnp.zeros_like(latent),
        )

        def store(buffer, value):
            return jnp.where(
                active, lax.dynamic_update_index_in_dim(buffer, value, slot, 0), buffer
            )

        return (
            stepped,
            store(saved_pad, latent_pad),
            store(saved_sum, group_sum),
            store(saved_square, squares),
            store(path, stepped),
        )

    start_carry = (
        jnp.zeros_like(noise[0]),
        jnp.zeros((micro_count, channels, row_count + 2, breadth), jnp.float32),
        jnp.zeros((micro_count, GROUPS), jnp.float32),
        jnp.zeros((micro_count, GROUPS), jnp.float32),
        jnp.zeros_like(noise),
    )
    _, saved_pad, saved_sum, saved_square, path = lax.fori_loop(0, ticks, forward_tick, start_carry)

    def backward_tick(tick, carry):
        outgoing, grad_total = carry
        arrived = passed_along(outgoing, "section", -1)
        micro_index = tick - (sections - 1 - section_index)
        active = (micro_index >= 0) & (micro_index < micro_count)
        slot = jnp.clip(micro_index, 0, micro_count - 1)
        latent_pad = lax.dynamic_index_in_dim(saved_pad, slot, 0, keepdims=False)
        group_sum = lax.dynamic_index_in_dim(saved_sum, slot, 0, keepdims=False)
        squares = lax.dynamic_index_in_dim(saved_square, slot, 0, keepdims=False)
        finished = lax.dynamic_index_in_dim(
            path, slot, 0, keepdims=False
        ) - lax.dynamic_index_in_dim(target, slot, 0, keepdims=False)
        adjoint = jnp.where(section_index == sections - 1, finished, arrived)

        def pulled():
            (projected, activated), pre_pull = jax.vjp(prepare, latent_pad, group_sum, squares)
            blank = jnp.zeros((row_count, breadth, features), jnp.float32)
            _, post_pull = jax.vjp(finish, latent_pad, projected, blank)
            pad_first, proj_grad, conv_grad = post_pull(adjoint)
            act_grad = jnp.zeros_like(activated)
            weight_parts = []
            for offset in range(9):
                shift_row = offset // 3
                shift_col = offset % 3
                window = activated[
                    shift_row : shift_row + row_count, shift_col : shift_col + breadth
                ]
                back = jnp.einsum("rwd,cd->rwc", conv_grad, wide_conv[offset], precision=precise)
                act_grad = act_grad.at[
                    shift_row : shift_row + row_count, shift_col : shift_col + breadth
                ].add(back)
                weight_parts.append(jnp.einsum("rwc,rwd->cd", window, conv_grad, precision=precise))
            pad_second, sum_grad, square_grad = pre_pull((proj_grad, act_grad))
            return (
                pad_first + pad_second,
                sum_grad,
                square_grad,
                grad_total + jnp.stack(weight_parts),
            )

        def skipped():
            return (
                jnp.zeros_like(latent_pad),
                jnp.zeros_like(group_sum),
                jnp.zeros_like(squares),
                grad_total,
            )

        pad_grad, sum_grad, square_grad, grad_total = lax.cond(active, pulled, skipped)
        rims = jnp.concatenate([pad_grad[:, :1], pad_grad[:, -1:]], axis=1)
        moved = exchange_rows(rims)
        sum_total, square_total = total_stats((sum_grad, square_grad))
        _, stat_pull = jax.vjp(
            lambda own_rows: group_partial(own_rows, w_in, GROUPS), latent_pad[:, 1:-1]
        )
        own_grad = stat_pull((sum_total, square_total))[0]
        result = pad_grad[:, 1:-1] + own_grad
        result = result.at[:, 0].add(moved[:, 0]).at[:, -1].add(moved[:, 3])
        return (jnp.where(active, result, 0.0), grad_total)

    _, grad_total = lax.fori_loop(
        0, ticks, backward_tick, (jnp.zeros_like(noise[0]), jnp.zeros_like(wide_conv))
    )
    partial_share = lax.psum_scatter(grad_total, "tensor", scatter_dimension=2, tiled=True)
    share = over_copies(partial_share, "section")
    return (path[None], share)


def solution(mesh):
    placed = (
        P(None, None, "tensor", None),
        P(None, None, "tensor", None),
        P(),
        P(),
        P(),
        P(),
        P(),
        P(),
        P(),
    )
    return jax.shard_map(
        local,
        mesh=mesh,
        in_specs=placed,
        out_specs=(P("section", None, None, "tensor", None), P(None, None, "tensor")),
        check_vma=False,
    )
```

profile of v0, /device:TPU:1, one launch (start us, length us, event | category | flops | bytes accessed | tf_op | source)
XLA Modules:
  0.0 1832.0 jit_solution(17152328028857552501)
XLA Ops:
  22.1 501.7 %while.55 = (s32[]{:T(128)}, f32[4,2,32]{2,0,1:T(4,128)}, f32[2,4,4,32]{3,1,2,0:T(4,128)S(1)}, f32[2,32]{1,0:T(2,128)S(1)}, f32[2,32]{1,0:T(2,128)S(1)}, /*index...) while((s32[]{:T(128)}, f32[4,2,32]{2,0,1:T(4,128)}, ...), condition=%wide.region_14.15_spmd.clone, body=%wide.region_6.14_spmd.clone.sunk | while | flops 122700736 | bytes 4886359 | solution.py:183
  47.8 12.7 conditional.6
  80.1 12.7 conditional.6
  116.8 17.2 collective-permute-start
  177.1 15.8 collective-permute-start
  236.8 13.1 collective-permute-start
  293.9 14.0 collective-permute-start
  351.8 13.1 collective-permute-start
  408.8 14.0 collective-permute-start
  466.8 13.1 collective-permute-start
  526.2 1084.4 %while.56 = (s32[]{:T(128)}, f32[4,2,32]{2,0,1:T(4,128)S(1)}, f32[9,320,320]{2,1,0:T(8,128)}, s32[]{:T(128)}, f32[2,4,4,32]{3,1,2,0:T(4,128)S(1)}, /*index=5*/f3...) while((s32[]{:T(128)}, f32[4,2,32]{2,0,1:T(4,128)S(1)}, ...), condition=%wide.region_24.25_spmd.clone, body=%wide.region_15.24_spmd.clone.sunk | while | flops 1424695552 | bytes 27102820 | solution.py:245
  527.6 16.0 collective-permute-done.3
  558.9 6.9 collective-permute-done.3
  566.5 6.2 all-to-all-start.1
  582.5 11.5 collective-permute-done.3
  594.7 6.2 all-to-all-start.1
  610.7 6.8 collective-permute-done.3
  618.3 6.2 all-to-all-start.1
  634.3 12.4 collective-permute-done.3
  647.4 6.2 all-to-all-start.1
  663.4 6.9 collective-permute-done.3
  671.0 6.2 all-to-all-start.1
  687.0 11.5 collective-permute-done.3
  699.2 6.2 all-to-all-start.1
  715.2 6.9 collective-permute-done.3
  722.8 6.2 all-to-all-start.1
  738.8 12.4 collective-permute-done.3
  751.9 6.2 all-to-all-start.1
  767.9 6.6 collective-permute-done.3
  775.2 6.2 all-to-all-start.1
  791.2 11.8 collective-permute-done.3
  803.6 6.2 all-to-all-start.1
  819.7 6.6 collective-permute-done.3
  827.0 6.2 all-to-all-start.1
  843.0 12.7 collective-permute-done.3
  856.3 6.2 all-to-all-start.1
  872.3 6.6 collective-permute-done.3
  879.6 6.2 all-to-all-start.1
  895.7 11.1 collective-permute-done.3
  907.5 6.2 all-to-all-start.1
  923.5 572.2 %collective-permute-done.3 = f32[4,2,32]{2,0,1:T(4,128)S(1)} collective-permute-done((f32[4,2,32]{2,0,1:T(4,128)S(1)}, f32[4,2,32]{2,0,1:T(4,128)S(1)}, u32[]{:S(2)}, u32[]{:S(2)}) %collective-permute-start.3) | collective-permute-done | bytes 1056 | tf_op jit(solution)/shard_map/while/body/eval_jaxpr/ppermute | solution.py:52
  1495.7 38.1 %conditional.7 = (f32[4,4,32]{2,0,1:T(4,128)S(1)}, f32[32]{0:T(128)S(1)}, f32[32]{0:T(128)S(1)}, f32[9,320,320]{2,1,0:T(8,128)}) conditional(s32[]{:T(128)} %convert_element_type.74, f32[9,320,320]{2,1,0:T(8,128)} %get-tuple-element.1782, (f32[]{:T(128)}, pred[]{:T(512)}, f32[2,4,2,32]{3,1,2,0:T(4,128)S(1)}, s32[]{:T(128)}, ...), branch_computations={%region_16.16_spmd, %region_17.22_spmd} | conditional | flops 1422665984 | bytes 26852650 | solution.py:233
  1550.5 6.6 collective-permute-done.3
  1557.2 38.1 %conditional.7 = (f32[4,4,32]{2,0,1:T(4,128)S(1)}, f32[32]{0:T(128)S(1)}, f32[32]{0:T(128)S(1)}, f32[9,320,320]{2,1,0:T(8,128)}) conditional(s32[]{:T(128)} %convert_element_type.74, f32[9,320,320]{2,1,0:T(8,128)} %get-tuple-element.1782, (f32[]{:T(128)}, pred[]{:T(512)}, f32[2,4,2,32]{3,1,2,0:T(4,128)S(1)}, s32[]{:T(128)}, ...), branch_computations={%region_16.16_spmd, %region_17.22_spmd} | conditional | flops 1422665984 | bytes 26852650 | solution.py:233
  1610.6 9.0 copy.32
  1619.6 68.1 %reduce-scatter.2.cloned.1.call-done = f32[9,320,20]{1,0,2:T(8,128)} async-done(((f32[9,320,320]{1,0,2:T(8,128)}), f32[9,320,20]{1,0,2:T(8,128)}) %reduce-scatter.2.cloned.1.call-update) | async-done | bytes 230416 | tf_op jit(solution)/shard_map/reduce_scatter | solution.py:248
  1691.5 9.0 all-to-all-start.2
  1701.2 120.4 %all-to-all-done.2 = f32[16,9,320,20]{2,3,1,0:T(8,128)} async-done(((f32[16,9,320,20]{2,3,1,0:T(8,128)}), f32[16,9,320,20]{2,3,1,0:T(8,128)}, u32[]{:S(2)}, u32[]{:S(2)}) %all-to-all-start.2) | async-done | bytes 3686432 | tf_op jit(solution)/shard_map/all_to_all | solution.py:33
  (1120 shorter events, 701.2 us)
Async XLA Ops:
  7.2 1680.5 %reduce-scatter.2.cloned.1.call-start = ((), (), s32[]{:S(2)}) async-start(), calls=%async_computation.4 | async-start | bytes 8355840 | tf_op jit(solution)/shard_map/reduce_scatter | solution.py:248
  28.5 13.6 collective-permute-start.1
  62.7 11.7 collective-permute-start.1
  98.8 11.7 collective-permute-start.1
  116.8 18.1 collective-permute-start
  135.0 11.7 collective-permute-start.1
  159.0 11.7 collective-permute-start.1
  177.1 16.7 collective-permute-start
  193.8 11.7 collective-permute-start.1
  218.8 11.7 collective-permute-start.1
  236.8 14.0 collective-permute-start
  250.8 11.7 collective-permute-start.1
  275.8 11.7 collective-permute-start.1
  293.9 14.9 collective-permute-start
  308.8 11.7 collective-permute-start.1
  333.8 11.7 collective-permute-start.1
  351.8 14.0 collective-permute-start
  365.8 11.7 collective-permute-start.1
  390.8 11.7 collective-permute-start.1
  408.8 14.9 collective-permute-start
  423.8 11.7 collective-permute-start.1
  448.8 11.7 collective-permute-start.1
  466.8 14.0 collective-permute-start
  480.8 11.7 collective-permute-start.1
  505.8 11.7 collective-permute-start.1
  526.2 17.4 collective-permute-start.3
  566.5 11.7 all-to-all-start.1
  581.2 12.9 collective-permute-start.3
  594.7 11.7 all-to-all-start.1
  618.3 11.7 all-to-all-start.1
  633.0 13.8 collective-permute-start.3
  647.4 11.7 all-to-all-start.1
  671.0 11.7 all-to-all-start.1
  685.7 12.8 collective-permute-start.3
  699.2 11.7 all-to-all-start.1
  722.8 11.7 all-to-all-start.1
  737.5 13.7 collective-permute-start.3
  751.9 11.7 all-to-all-start.1
  775.2 11.7 all-to-all-start.1
  789.8 13.1 collective-permute-start.3
  803.6 11.7 all-to-all-start.1
  827.0 11.7 all-to-all-start.1
  841.6 14.0 collective-permute-start.3
  856.3 11.7 all-to-all-start.1
  894.3 12.5 collective-permute-start.3
  907.5 11.7 all-to-all-start.1
  922.1 573.6 %collective-permute-start.3 = (f32[4,2,32]{2,0,1:T(4,128)S(1)}, f32[4,2,32]{2,0,1:T(4,128)S(1)}, u32[]{:S(2)}, u32[]{:S(2)}) collective-permute-start(f32[4,2,32]{2,0,1:T(4,128)S(1)} %broadcast_select_fusion.8), channel_id=1, source_target_pairs={{16,0},{32,16},{48,32},{64,48},{80,64},{96,80},{112,96},{128,112},... | collective-permute-start | bytes 3080 | tf_op jit(solution)/shard_map/while/body/eval_jaxpr/ppermute | solution.py:52
  1691.5 130.0 %all-to-all-start.2 = ((f32[16,9,320,20]{2,3,1,0:T(8,128)}), f32[16,9,320,20]{2,3,1,0:T(8,128)}, u32[]{:S(2)}, u32[]{:S(2)}) async-start(f32[16,9,320,20]{2,3,1,0:T(8,128)} %broadcast_in_dim.155), calls=%async_computation.3 | async-start | bytes 10616832 | tf_op jit(solution)/shard_map/all_to_all | solution.py:33
  (96 other events, 733.0 us)
Sparse Core Ops, SparseCore 0:
  1619.8 67.9 reduce-scatter.1
where the time goes:
time: 1840 us; the launch traced here: 1830 us
  waiting for transfers between devices  1050 us (57%)
  starting transfers between devices  557 us (30%)
  matrix products  91.7 us (5%)
  local copies, waits for them, and re-layouts  75.7 us (4%)
  other arithmetic  35 us (2%)
    ppermute x34, waiting for transfers between devices, passed_along(): return lax.ppermute(block, axis, route)  741 us
    all_to_all x35, waiting for transfers between devices, from_everyone(): lax.all_to_all(jnp.broadcast_to(x[None], (size, *x.shape)), axis, 0, 0, t...  212 us
    all_to_all x35, starting transfers between devices, from_everyone(): lax.all_to_all(jnp.broadcast_to(x[None], (size, *x.shape)), axis, 0, 0, t...  194 us
    ppermute x34, starting transfers between devices, passed_along(): return lax.ppermute(block, axis, route)  175 us
    ppermute x34, starting transfers between devices, extended(): lax.ppermute(tail, axis, [(i, (i + 1) % count) for i in range(ends)])  97.7 us
    ppermute x34, starting transfers between devices, extended(): lax.ppermute(head, axis, [((i + 1) % count, i) for i in range(ends)])  90.5 us
    reduce_scatter x1, waiting for transfers between devices, local(): lax.psum_scatter(grad_total, 'tensor', scatter_dimension=2, tiled=True)  68.1 us
  transfers between devices with their start and end apart: 138, of which 70 were waited for; matrix products, arithmetic and copies ran while one was open for 2% of the time, Pallas kernels for 0%

commit v1 on v0

v1 whole, which is shorter than its diff:
```python
import math

import jax
import jax.numpy as jnp
import numpy as np
from jax import lax
from jax.experimental import pallas as pl
from jax.experimental.pallas import tpu as pltpu
from jax.sharding import PartitionSpec as P


GROUPS = 32
STEPS = 16
CH = 4
C = 320
SIDE = 32
PIX = SIDE * SIDE
TILE = 256
F32 = jnp.float32
BF16 = jnp.bfloat16
EPS = 1e-05


def schedule_tables():
    grid = np.arange(1000, dtype=np.float64)
    low, high = math.sqrt(0.00085), math.sqrt(0.012)
    bar = np.cumprod(1.0 - (low + grid * ((high - low) / 999.0)) ** 2)
    table = np.zeros((3, 1024), np.float32)
    table[0, :1000] = np.sqrt(bar)
    table[1, :1000] = 1.0 / np.sqrt(bar)
    table[2, :1000] = np.sqrt(1.0 - bar)
    return table


def split(x, parts):
    out = []
    for _ in range(parts):
        head = x.astype(BF16)
        out.append(head)
        x = x - head.astype(F32)
    return out


def dot(a, b, dims=((1,), (0,)), precision=None):
    return lax.dot_general(a, b, (dims, ((), ())), precision=precision, preferred_element_type=F32)


NT = ((1,), (1,))


def rolled(x, shift, axis):
    return pltpu.roll(x, shift % x.shape[axis], axis)


def doubled(x):
    return jnp.concatenate([x, x], axis=0)


def row_index(shape):
    return lax.broadcasted_iota(jnp.int32, shape, 0)


def prepare_kernel(feat, w1, w2t, w_conv, w_out_t, w_in, w_fwd, w_bwd, emb, rows, cols):
    hi = lax.Precision.HIGHEST
    out8 = doubled(w_out_t[...])
    in8 = doubled(w_in[...])
    hidden = dot(feat[...], w1[...], precision=hi)
    hidden = hidden * jax.nn.sigmoid(hidden)
    embed = dot(hidden, w2t[...], NT, precision=hi)
    shift = dot(out8, embed, NT, precision=hi)
    for s in range(STEPS):
        emb[s] = jnp.broadcast_to(shift[:, s : s + 1], (8, 128))
    parts = split(out8, 3)
    stacked = jnp.concatenate([p.astype(F32) for p in parts] + [jnp.zeros_like(out8)], axis=0).astype(BF16)
    is_head = row_index((8, C)) < CH
    heads, tails, mixed = [], [], []
    for tap in range(9):
        got = dot(stacked, w_conv[tap], NT)
        full = got[0:8] + got[8:16] + got[16:24]
        head = full.astype(BF16).astype(F32)
        tail = full - head
        mixed.append(jnp.where(is_head, head, tail))
        heads.append(head)
        tails.append(tail)
    pad = jnp.zeros((8, C), F32)
    w_fwd[...] = jnp.concatenate(mixed + [pad], axis=0).astype(BF16)
    both = jnp.concatenate(heads + tails, axis=0)
    w_bwd[...] = both.T.astype(BF16)
    first = row_index((8, C)) < CH
    next1, next2 = rolled(in8, -1, 0), rolled(in8, -2, 0)
    top = jnp.where(first, in8, in8 * in8)
    low = in8 * jnp.where(first, 2.0 * next1, next2)
    a = lax.broadcasted_iota(jnp.int32, (C, C), 0) // (C // GROUPS)
    b = lax.broadcasted_iota(jnp.int32, (C, C), 1) // (C // GROUPS)
    member = (a == b).astype(F32)
    sums = dot(jnp.concatenate([top, low], axis=0), member, precision=hi)
    rows[...] = sums * (1.0 / (PIX * (C // GROUPS)))
    for j in range(CH):
        ahead = jnp.sum(out8 * rolled(in8, -j, 0), axis=1, keepdims=True)
        back = jnp.sum(rolled(out8, -j, 0) * in8, axis=1, keepdims=True)
        cols[j] = jnp.broadcast_to(ahead, (8, 128))
        cols[CH + j] = jnp.broadcast_to(back, (8, 128))


def prepare(feat, w1, w2t, w_conv, w_out_t, w_in):
    return pl.pallas_call(
        prepare_kernel,
        out_shape=(
            jax.ShapeDtypeStruct((80, C), BF16),
            jax.ShapeDtypeStruct((C, 144), BF16),
            jax.ShapeDtypeStruct((STEPS, 8, 128), F32),
            jax.ShapeDtypeStruct((16, C), F32),
            jax.ShapeDtypeStruct((8, 8, 128), F32),
        ),
        name="prepare",
    )(feat, w1, w2t, w_conv, w_out_t, w_in)


def wide(col):
    return jnp.concatenate([col] * (PIX // 128), axis=1)


def chain_kernel(
    place, times, table, recv, w_fwd, w_bwd, emb, rows, cols, gain, w_in,
    sent, lat, stat, act, slope, taps, total,
):
    section, block = place[0], place[1]
    rid = row_index((8, PIX))
    upper = rid < CH
    lane = lax.broadcasted_iota(jnp.int32, (8, PIX), 1)
    column = lane % SIDE
    not_left, not_right = column > 0, column < SIDE - 1
    not_top, not_bottom = lane >= SIDE, lane < PIX - SIDE
    srow = row_index((8, C))
    supper = srow < CH
    in8 = doubled(w_in[...])
    in5 = jnp.where(supper, in8, 0.0)
    half_gain = 0.5 * gain[...]

    start = jnp.concatenate([recv[i] for i in range(16)], axis=1)
    latent0 = jnp.where(upper, start, rolled(start, 4, 0))
    target8 = jnp.where(upper, rolled(start, 4, 0), start)

    def coefs(s):
        now = times[s]
        last = s == STEPS - 1
        after = times[jnp.minimum(s + 1, STEPS - 1)]
        root = jnp.where(last, 1.0, table[0, after])
        rest = jnp.where(last, 0.0, table[2, after])
        keep = root * table[1, now]
        return keep, rest - keep * table[2, now]

    def homogeneous(l8):
        return jnp.where(upper, l8, jnp.where(rid == CH, 1.0, 0.0))

    def forward(s, l8):
        keep, nc = coefs(s)
        lat[s] = l8
        r1, r2, r3 = rolled(l8, -1, 0), rolled(l8, -2, 0), rolled(l8, -3, 0)
        x0 = jnp.where(upper, l8, l8 * l8)
        x1 = l8 * jnp.where(upper, r1, r2)
        m0 = jnp.sum(x0, axis=1, keepdims=True)
        m1 = jnp.sum(x1, axis=1, keepdims=True)
        p0 = rows[0:8] * m0
        p1 = rows[8:16] * m1
        avg = jnp.sum(jnp.where(supper, p0, 0.0), axis=0, keepdims=True)
        sq = jnp.sum(jnp.where(supper, 0.0, p0) + p1, axis=0, keepdims=True)
        rstd = lax.rsqrt(sq - avg * avg + EPS)
        scale = rstd * half_gain
        stat[s, 0:1] = avg
        stat[s, 1:2] = rstd
        stat[s, 2:3] = scale
        wz = jnp.where(srow == CH, -avg * scale, in5 * scale)
        a, b, c = [p.astype(F32) for p in split(wz, 3)]
        wzs = jnp.concatenate([a, a, b, b, a, c], axis=0).T.astype(BF16)
        d, e, f = [p.astype(F32) for p in split(homogeneous(l8), 3)]
        ls = jnp.concatenate([d, e, d, e, f, d], axis=0).astype(BF16)
        linear = (
            wide(cols[0]) * l8 + wide(cols[1]) * r1 + wide(cols[2]) * r2 + wide(cols[3]) * r3
        )
        linear = keep * l8 + nc * (linear + wide(emb[s]))
        for j in range(PIX // TILE):
            at = slice(j * TILE, (j + 1) * TILE)
            h = dot(wzs, ls[:, at])
            t = jnp.tanh(h)
            u = h * t
            narrow = (h + u).astype(BF16)
            act[s, :, at] = narrow
            slope[s, :, at] = (1.0 + t) + (h - u * t)
            taps[:, at] = dot(w_fwd[...], narrow)

        def tap(dy, dx):
            k = 8 * (3 * dy + dx)
            return taps[k : k + 8]

        def column_sum(dx):
            above = jnp.where(not_top, rolled(tap(0, dx), SIDE, 1), 0.0)
            below = jnp.where(not_bottom, rolled(tap(2, dx), -SIDE, 1), 0.0)
            return tap(1, dx) + above + below

        conv = column_sum(1)
        conv = conv + jnp.where(not_left, rolled(column_sum(0), 1, 1), 0.0)
        conv = conv + jnp.where(not_right, rolled(column_sum(2), -1, 1), 0.0)
        conv = conv + rolled(conv, 4, 0)
        return linear + nc * conv

    final = lax.fori_loop(0, STEPS, forward, latent0)
    lat[STEPS] = final
    total[...] = jnp.zeros_like(total)

    def backward(i, adj):
        s = STEPS - 1 - i
        keep, nc = coefs(s)
        l8 = lat[s]
        avg, rstd, scale = stat[s, 0:1], stat[s, 1:2], stat[s, 2:3]
        ng = nc * adj
        head = ng.astype(BF16).astype(F32)
        x = jnp.where(upper, head, ng - head)
        shifted = []
        sides = (
            jnp.where(not_right, rolled(x, -1, 1), 0.0),
            x,
            jnp.where(not_left, rolled(x, 1, 1), 0.0),
        )
        for y in sides:
            shifted.append(jnp.where(not_bottom, rolled(y, -SIDE, 1), 0.0))
        shifted.extend(sides)
        for y in sides:
            shifted.append(jnp.where(not_top, rolled(y, SIDE, 1), 0.0))
        col = jnp.concatenate(shifted + shifted, axis=0).astype(BF16)
        ws = in8 * scale
        whead = ws.astype(BF16).astype(F32)
        wd = jnp.where(supper, whead, ws - whead).astype(BF16)
        d, e = [p.astype(F32) for p in split(homogeneous(l8), 2)]
        ls = jnp.concatenate([d, e], axis=0).astype(BF16)
        direct = []
        sx = jnp.zeros((16, C), F32)
        grad = jnp.zeros((72, C), F32)
        for j in range(PIX // TILE):
            at = slice(j * TILE, (j + 1) * TILE)
            g = dot(w_bwd[...], col[:, at]) * slope[s, :, at]
            g0, g1 = split(g, 2)
            direct.append(dot(wd, g0) + dot(wd, g1))
            sx = sx + dot(ls[:, at], g0, NT) + dot(ls[:, at], g1, NT)
            grad = grad + dot(col[:72, at], act[s, :, at], NT)
        total[...] += grad
        dl = jnp.concatenate(direct, axis=1)
        dl = dl + rolled(dl, 4, 0)
        sx = sx[0:8] + sx[8:16]
        s1 = sx[CH : CH + 1]
        lw = jnp.sum(in5 * sx, axis=0, keepdims=True)
        q = (-0.5 * rstd * rstd * rstd) * half_gain * (lw - avg * s1)
        da = -scale * s1 - 2.0 * avg * q
        c0 = jnp.sum(rows[0:8] * jnp.where(supper, da, q), axis=1, keepdims=True)
        c1 = jnp.sum(rows[8:16] * q, axis=1, keepdims=True)
        c0 = jnp.broadcast_to(c0, (8, 128))
        c1 = jnp.broadcast_to(c1, (8, 128))
        up8 = upper[:, :128]
        c0r, c1r = rolled(c0, 4, 0), rolled(c1, 4, 0)
        dm = jnp.where(up8, c0, c0r)
        d0 = 2.0 * jnp.where(up8, c0r, c0)
        d1 = jnp.where(up8, c1, c1r)
        d3 = rolled(d1, 1, 0)
        d2 = jnp.where(up8, c1r, c1)
        d2 = d2 + rolled(d2, 2, 0)
        r1, r2, r3 = rolled(l8, -1, 0), rolled(l8, -2, 0), rolled(l8, -3, 0)
        stats = wide(dm) + wide(d0) * l8 + wide(d1) * r1 + wide(d2) * r2 + wide(d3) * r3
        a1, a2, a3 = rolled(adj, -1, 0), rolled(adj, -2, 0), rolled(adj, -3, 0)
        linear = (
            wide(cols[4]) * adj + wide(cols[5]) * a1 + wide(cols[6]) * a2 + wide(cols[7]) * a3
        )
        return keep * adj + nc * linear + dl + stats

    lax.fori_loop(0, STEPS, backward, final - target8)
    for k in range(9):
        part = total[8 * k : 8 * k + 8]
        part = part + rolled(part, 4, 0)
        sent[4 * k : 4 * k + 4] = part[0:4]
    mine = lat[section + 1, :, pl.ds(pl.multiple_of(block * 128, 128), 128)]
    sent[36:40] = jnp.concatenate([mine[0:4], jnp.zeros((4, C - 128), F32)], axis=1)


def chain(place, times, table, recv, w_fwd, w_bwd, emb, rows, cols, gain, w_in):
    smem = pl.BlockSpec(memory_space=pltpu.SMEM)
    vmem = pl.BlockSpec(memory_space=pltpu.VMEM)
    return pl.pallas_call(
        chain_kernel,
        out_shape=jax.ShapeDtypeStruct((40, C), F32),
        in_specs=[smem] * 3 + [vmem] * 8,
        out_specs=vmem,
        scratch_shapes=[
            pltpu.VMEM((STEPS + 1, 8, PIX), F32),
            pltpu.VMEM((STEPS, 8, C), F32),
            pltpu.VMEM((STEPS, C, PIX), BF16),
            pltpu.VMEM((STEPS, C, PIX), F32),
            pltpu.VMEM((80, PIX), F32),
            pltpu.VMEM((72, C), F32),
        ],
        name="chain",
    )(place, times, table, recv, w_fwd, w_bwd, emb, rows, cols, gain, w_in)


def finish_kernel(place, own, other, w_out_t, path, grad):
    core = place[2]
    hi = lax.Precision.HIGHEST
    mine = own[36:40, 0:128]
    theirs = other[36:40, 0:128]
    first = jnp.where(core == 0, mine, rolled(theirs, 64, 1))
    second = jnp.where(core == 0, theirs, rolled(mine, 64, 1))
    for m, x in enumerate((first, second)):
        for c in range(CH):
            for r in range(2):
                path[0, m, c, r : r + 1] = x[c : c + 1, SIDE * r : SIDE * r + SIDE]
    both = own[0:36] + other[0:36]
    for k in range(9):
        grad[k] = dot(w_out_t[...], both[4 * k : 4 * k + 4], precision=hi)


def finish(place, own, other, w_out_rows):
    smem = pl.BlockSpec(memory_space=pltpu.SMEM)
    vmem = pl.BlockSpec(memory_space=pltpu.VMEM)
    width = w_out_rows.shape[0]
    return pl.pallas_call(
        finish_kernel,
        out_shape=(
            jax.ShapeDtypeStruct((1, 2, CH, 2, SIDE), F32),
            jax.ShapeDtypeStruct((9, width, C), F32),
        ),
        in_specs=[smem] + [vmem] * 3,
        out_specs=(vmem, vmem),
        name="finish",
    )(place, own, other, w_out_rows)


def features(times):
    half = C // 2
    frequency = jnp.exp(-math.log(10000.0) * jnp.arange(half, dtype=F32) / half)
    angles = times.astype(F32)[:, None] * frequency[None]
    return jnp.concatenate([jnp.cos(angles), jnp.sin(angles)], axis=1)


def local(noise, target, timesteps, w_in, gn_gain, w_time1, w_time2, w_conv, w_out):
    count = lax.axis_size("tensor")
    index = lax.axis_index("tensor")
    place = jnp.stack([lax.axis_index("section"), index // 2, index % 2]).astype(jnp.int32)
    both = jnp.concatenate([noise.reshape(2, CH, 2 * SIDE), target.reshape(2, CH, 2 * SIDE)], axis=1)
    packed = jnp.tile(both, (count // 2, 1, 1))
    recv = lax.all_to_all(packed, "tensor", 0, 0, tiled=True)
    w_out_t = w_out.T
    made = prepare(features(timesteps), w_time1, w_time2.T, w_conv, w_out_t, w_in)
    own = chain(place, timesteps, jnp.asarray(schedule_tables()), recv, *made, gn_gain[None], w_in)
    other = lax.ppermute(own, "tensor", [(i, i ^ 1) for i in range(count)])
    width = C // count
    share = lax.dynamic_slice_in_dim(w_out, index * width, width, axis=0)
    path, grad = finish(place, own, other, share)
    return path, jnp.swapaxes(grad, 1, 2)


def solution(mesh):
    placed = (
        P(None, None, "tensor", None),
        P(None, None, "tensor", None),
        P(),
        P(),
        P(),
        P(),
        P(),
        P(),
        P(),
    )
    return jax.shard_map(
        local,
        mesh=mesh,
        in_specs=placed,
        out_specs=(P("section", None, None, "tensor", None), P(None, None, "tensor")),
        check_vma=False,
    )
```

time: 1840 us -> 81.5 us (0.04)
  waiting for transfers between devices: 1050 us -> 0.01 us
  starting transfers between devices: 557 us -> 7.02 us
  matrix products: 91.7 us -> 0 us
  local copies, waits for them, and re-layouts: 75.7 us -> 6.87 us
  Pallas kernels: 0 us -> 63.7 us
  other arithmetic: 35 us -> 2.86 us
    ppermute x102 -> x1, waiting for transfers between devices: 772 us -> 0.01 us  [local(): other = lax.ppermute(own, 'tensor', [(i, i ^ 1) for i in range(count)])]
    ppermute x102 -> x1, starting transfers between devices: 363 us -> 0.12 us  [local(): other = lax.ppermute(own, 'tensor', [(i, i ^ 1) for i in range(count)])]
    all_to_all x35 -> x1, waiting for transfers between devices: 212 us -> 0.01 us  [local(): recv = lax.all_to_all(packed, 'tensor', 0, 0, tiled=True)]
    all_to_all x35 -> x1, starting transfers between devices: 194 us -> 6.9 us  [local(): recv = lax.all_to_all(packed, 'tensor', 0, 0, tiled=True)]
    dot_general x117 -> x0, matrix products: 91.7 us -> none  [the longest x18 35.4 us: pulled(): jnp.einsum('rwd,cd->rwc', conv_grad, wide_conv[offset], precision=precise)]
    reduce_scatter x1 -> x0, waiting for transfers between devices: 68.1 us -> none  [local(): lax.psum_scatter(grad_total, 'tensor', scatter_dimension=2, tiled=True)]
    pallas_call x0 -> x3, Pallas kernels: none -> 63.7 us  [the longest x1 54 us: chain(): pl.pallas_call(chain_kernel, out_shape=jax.ShapeDtypeStruct((40, C), F32)...]
    broadcast_in_dim x129 -> x1, local copies, waits for them, and re-layouts: 32.5 us -> 1.24 us  [local(): gn_gain[None]]
  transfers between devices with their start and end apart: 138 -> 2, of which waited for: 70 -> 0; matrix products, arithmetic and copies ran while one was open for 2% -> 6% of each run, Pallas kernels for 0% -> 9%
where the time goes in v1:
time: 81.5 us; the launch traced here: 81.2 us
  Pallas kernels  63.7 us (78%)
  starting transfers between devices  7.02 us (9%)
  local copies, waits for them, and re-layouts  6.87 us (8%)
  other arithmetic  2.86 us (4%)
    pallas_call x1, Pallas kernels, chain(): pl.pallas_call(chain_kernel, out_shape=jax.ShapeDtypeStruct((40, C), F32)...  54 us
    pallas_call x1, Pallas kernels, prepare(): pl.pallas_call(prepare_kernel, out_shape=(jax.ShapeDtypeStruct((80, C), B...  7.6 us
    all_to_all x1, starting transfers between devices, local(): recv = lax.all_to_all(packed, 'tensor', 0, 0, tiled=True)  6.9 us
    unnamed x5, local copies, waits for them, and re-layouts  2.72 us
    pallas_call x1, Pallas kernels, finish(): pl.pallas_call(finish_kernel, out_shape=(jax.ShapeDtypeStruct((1, 2, CH,...  2.16 us
  transfers between devices with their start and end apart: 2, of which 0 were waited for; matrix products, arithmetic and copies ran while one was open for 6% of the time, Pallas kernels for 9%

profile of v1, /device:TPU:1, one launch (start us, length us, event | category | flops | bytes accessed | tf_op | source)
XLA Modules:
  0.0 81.2 jit_solution(2229452718781335258)
XLA Ops:
  0.6 0.8 reshape.20
  1.4 0.8 reshape.21
  2.2 0.7 reshape.22
  2.9 6.9 %all-to-all-start = ((f32[16,1,512]{2,1,0:T(1,128)}), f32[16,1,512]{2,1,0:T(1,128)S(1)}, u32[]{:S(2)}, u32[]{:S(2)}) async-start(f32[16,1,512]{2,1,0:T(1,128)} %reshape.22), calls=%async_computation | async-start | bytes 65536 | tf_op jit(solution)/shard_map/all_to_all | solution.py:348
  9.8 0.7 convert_element_type.3
  10.5 0.1 multiply_cosine_fusion
  10.7 0.7 pad_maximum_fusion.feat
  11.3 0.6 pad_add_fusion.place
  11.9 1.2 %broadcast_in_dim.2.gain = f32[1,320]{1,0:T(1,128)} reshape(f32[320]{0:T(512)} %param.14) | data formatting | bytes 2560 | tf_op jit(solution)/shard_map/broadcast_in_dim | solution.py:351
  13.2 7.6 %prepare.1 = (bf16[80,320]{1,0:T(8,128)(2,1)}, bf16[320,144]{1,0:T(8,128)(2,1)}, f32[16,8,128]{2,1,0:T(8,128)}, f32[16,320]{1,0:T(8,128)}, f32[8,8,128]{2,1,0:T(8,128)}) custom-call(f32[16,320]{1,0:T(8,128)} %pad_maximum_fusion.feat, f32[320,1280]{1,0:T(8,128)} %w1.1, f32[320,1280]{1,0:T(8,128)} %bitcast.7, bf16[9,320,320]{2,1,0:T(8,128)(2,1)} %w_conv.1, ...), custom_call_target="tpu_custom_call" | custom-call | tf_op jit(solution)/shard_map/prepare/pallas_call | solution.py:106
  20.8 0.0 all-to-all-done
  20.8 0.6 broadcast.13
  21.4 0.8 reduce
  22.1 0.7 reshape.23.recv
  22.8 54.0 %chain.1.own = f32[40,320]{1,0:T(8,128)} custom-call(s32[3]{0:T(128)} %pad_add_fusion.place, s32[16]{0:T(128)} %times.1, f32[3,1024]{1,0:T(4,128)} %constant.43.clone.table, f32[16,8,64]{2,1,0:T(8,128)} %reshape.23.recv, bf16[80,320]{1,0:T(8,128)(2,1)} %get-tuple-element.9.w_fwd, bf16[320,144]{1,0:T(8,128)(2,1)} %get-tuple-element.10.w_bwd, ...), custom_call_target="tpu_custom_call" | custom-call | tf_op jit(solution)/shard_map/chain/pallas_call | solution.py:286
  76.8 0.1 collective-permute-start
  76.9 0.8 constant_dynamic-slice_fusion
  77.7 0.7 copy.13.w_out_t
  78.4 0.0 collective-permute-done.other
  78.4 0.0 copy-start
  78.4 0.6 copy-done
  79.0 2.2 %finish.1 = (f32[1,2,4,2,32]{4,3,2,1,0:T(2,128)}, f32[9,20,320]{2,1,0:T(8,128)}) custom-call(s32[3]{0:T(128)} %pad_add_fusion.place, f32[40,320]{1,0:T(8,128)} %chain.1.own, f32[40,320]{1,0:T(8,128)} %copy-done, f32[20,4]{1,0:T(8,128)} %copy.13.w_out_t), custom_call_target="tpu_custom_call" | custom-call | tf_op jit(solution)/shard_map/finish/pallas_call | solution.py:323
  (3 shorter events, 0.0 us)
Async XLA Ops:
  2.9 17.9 %all-to-all-start = ((f32[16,1,512]{2,1,0:T(1,128)}), f32[16,1,512]{2,1,0:T(1,128)S(1)}, u32[]{:S(2)}, u32[]{:S(2)}) async-start(f32[16,1,512]{2,1,0:T(1,128)} %reshape.22), calls=%async_computation | async-start | bytes 65536 | tf_op jit(solution)/shard_map/all_to_all | solution.py:348
  76.8 1.6 %collective-permute-start = (f32[40,320]{1,0:T(8,128)}, f32[40,320]{1,0:T(8,128)S(1)}, u32[]{:S(2)}, u32[]{:S(2)}) collective-permute-start(f32[40,320]{1,0:T(8,128)} %chain.1.own), channel_id=1, source_target_pairs={{0,1},{1,0},{2,3},{3,2},{4,5},{5,4},{6,7},{7,6},{8,9},{9,8},{10,11... | collective-permute-start | bytes 153608 | tf_op jit(solution)/shard_map/ppermute | solution.py:352
  78.4 0.6 copy-start

commit v2 on v1

v2 whole, which is shorter than its diff:
```python
import math

import jax
import jax.numpy as jnp
import numpy as np
from jax import lax
from jax.experimental import pallas as pl
from jax.experimental.pallas import tpu as pltpu
from jax.sharding import PartitionSpec as P


GROUPS = 32
STEPS = 16
CH = 4
C = 320
SIDE = 32
PIX = SIDE * SIDE
TILE = 256
F32 = jnp.float32
BF16 = jnp.bfloat16
EPS = 1e-05


def schedule_tables():
    grid = np.arange(1000, dtype=np.float64)
    low, high = math.sqrt(0.00085), math.sqrt(0.012)
    bar = np.cumprod(1.0 - (low + grid * ((high - low) / 999.0)) ** 2)
    table = np.zeros((3, 1024), np.float32)
    table[0, :1000] = np.sqrt(bar)
    table[1, :1000] = 1.0 / np.sqrt(bar)
    table[2, :1000] = np.sqrt(1.0 - bar)
    return table


def split(x, parts):
    out = []
    for _ in range(parts):
        head = x.astype(BF16)
        out.append(head)
        x = x - head.astype(F32)
    return out


def dot(a, b, dims=((1,), (0,)), precision=None):
    return lax.dot_general(a, b, (dims, ((), ())), precision=precision, preferred_element_type=F32)


NT = ((1,), (1,))


def rolled(x, shift, axis):
    return pltpu.roll(x, shift % x.shape[axis], axis)


def doubled(x):
    return jnp.concatenate([x, x], axis=0)


def row_index(shape):
    return lax.broadcasted_iota(jnp.int32, shape, 0)


def position():
    return lax.axis_index("section"), lax.axis_index("tensor")


def wave_tables():
    half = C // 2
    f = np.exp(-math.log(10000.0) * np.arange(half, dtype=np.float64) / half)
    step = np.arange(32, dtype=np.float64)[:, None]
    big, small = 32.0 * step * f, step * f
    both = lambda a, b: np.concatenate([a, b], axis=1)
    return np.stack(
        [
            both(np.cos(big), np.sin(big)),
            both(-np.sin(big), np.cos(big)),
            both(np.cos(small), np.cos(small)),
            both(np.sin(small), np.sin(small)),
        ]
    ).astype(np.float32)


def pack_kernel(noise, target, packed):
    for m in range(2):
        parts = [x[m, :, r, :] for x in (noise, target) for r in range(2)]
        tile = jnp.concatenate(parts, axis=1)
        for j in range(8):
            packed[2 * j + m] = tile


def pack(noise, target):
    vmem = pl.BlockSpec(memory_space=pltpu.VMEM)
    return pl.pallas_call(
        pack_kernel,
        out_shape=jax.ShapeDtypeStruct((16, CH, 128), F32),
        in_specs=[vmem] * 2,
        out_specs=vmem,
        name="pack",
    )(noise, target)


def two(x):
    head = x.astype(BF16)
    return head, (x - head.astype(F32)).astype(BF16)


def stacked(a, b):
    return jnp.concatenate([a.astype(F32), b.astype(F32)], axis=0).astype(BF16)


def prepare_kernel(
    times, waves, w_out_t, w_in, gain, w1_hbm, w2t_hbm, conv_hbm,
    w_fwd, w_bwd, emb, rows, cols, w1, w2t, conv, sems,
):
    copies = [pltpu.make_async_copy(conv_hbm.at[k], conv.at[k], sems.at[k]) for k in range(9)]
    copies.append(pltpu.make_async_copy(w1_hbm, w1, sems.at[9]))
    copies.append(pltpu.make_async_copy(w2t_hbm, w2t, sems.at[10]))
    for c in copies:
        c.start()
    out8 = doubled(w_out_t[...])
    in8 = doubled(w_in[...])
    first = row_index((8, C)) < CH
    next1, next2 = rolled(in8, -1, 0), rolled(in8, -2, 0)
    top = jnp.where(first, in8, in8 * in8)
    low = in8 * jnp.where(first, 2.0 * next1, next2)
    group = lambda axis: lax.broadcasted_iota(jnp.int32, (C, C), axis) * 6554 >> 16
    member = jnp.where(group(0) == group(1), 1.0, 0.0).astype(BF16)
    both = jnp.concatenate([top, low], axis=0)
    p1, p2, p3 = [p.astype(F32) for p in split(both, 3)]
    sums = dot(jnp.concatenate([p1, p2, p3], axis=0).astype(BF16), member)
    sums = (sums[0:16] + sums[16:32] + sums[32:48]) * (1.0 / (PIX * (C // GROUPS)))
    rows[0:16] = sums
    for c in range(CH):
        rows[16 * (c + 1) : 16 * (c + 2)] = sums * w_in[c : c + 1]
    rows[80:88] = jnp.broadcast_to(0.5 * gain[...].reshape(1, C), (8, C))
    for j in range(CH):
        ahead = jnp.sum(out8 * rolled(in8, -j, 0), axis=1, keepdims=True)
        back = jnp.sum(rolled(out8, -j, 0) * in8, axis=1, keepdims=True)
        cols[j] = jnp.broadcast_to(ahead, (8, 128))
        cols[CH + j] = jnp.broadcast_to(back, (8, 128))
    repeated = jnp.concatenate([out8] * 16, axis=0).T
    lane = lax.broadcasted_iota(jnp.int32, (C, 128), 1)
    r_head, r_tail = two(repeated)
    r_head, r_tail = r_head.astype(F32), r_tail.astype(F32)
    acc = jnp.zeros((C, 256), F32)
    for k in range(9):
        copies[k].wait()
    for k in range(9):
        at = lane // 8 == k
        right = jnp.concatenate([jnp.where(at, r_head, 0.0), jnp.where(at, r_tail, 0.0)], axis=1)
        acc = acc + dot(conv[k], right.astype(BF16))
    full = acc[:, :128] + acc[:, 128:]
    head = full.astype(BF16).astype(F32)
    tail = full - head
    w_bwd[...] = jnp.concatenate([head[:, :80], tail[:, :80]], axis=1).astype(BF16)
    w_fwd[...] = jnp.where(lane % 8 < CH, head, tail).T[:80].astype(BF16)
    feats = []
    for s in range(STEPS):
        t = times[s]
        a, b = t >> 5, t & 31
        feats.append(
            waves[0, pl.ds(a, 1)] * waves[2, pl.ds(b, 1)]
            + waves[1, pl.ds(a, 1)] * waves[3, pl.ds(b, 1)]
        )
    f_head, f_tail = two(jnp.concatenate(feats, axis=0))
    o_head, o_tail = two(out8)
    copies[9].wait()
    w_head, w_tail = two(w1[...])
    z = dot(stacked(f_head, f_tail), w_head)
    z = 0.5 * (z[:STEPS] + z[STEPS:] + dot(f_head, w_tail))
    hidden = z + z * jnp.tanh(z)
    copies[10].wait()
    w_head, w_tail = two(w2t[...])
    y = dot(stacked(o_head, o_tail), w_head)
    y = y[0:8] + y[8:16] + dot(o_head, w_tail)
    y_head, y_tail = two(y)
    h_head, h_tail = two(hidden)
    x = dot(stacked(y_head, y_tail), h_head, NT)
    shift = x[0:8] + x[8:16] + dot(y_head, h_tail, NT)
    for s in range(STEPS):
        emb[s] = jnp.broadcast_to(shift[:, s : s + 1], (8, 128))


def prepare(times, w_out_t, w_in, gain, w1, w2t, w_conv):
    smem = pl.BlockSpec(memory_space=pltpu.SMEM)
    vmem = pl.BlockSpec(memory_space=pltpu.VMEM)
    hbm = pl.BlockSpec(memory_space=pl.ANY)
    return pl.pallas_call(
        prepare_kernel,
        out_shape=(
            jax.ShapeDtypeStruct((80, C), BF16),
            jax.ShapeDtypeStruct((C, 160), BF16),
            jax.ShapeDtypeStruct((STEPS, 8, 128), F32),
            jax.ShapeDtypeStruct((88, C), F32),
            jax.ShapeDtypeStruct((8, 8, 128), F32),
        ),
        in_specs=[smem] + [vmem] * 4 + [hbm] * 3,
        out_specs=(vmem,) * 5,
        scratch_shapes=[
            pltpu.VMEM(w1.shape, F32),
            pltpu.VMEM(w2t.shape, F32),
            pltpu.VMEM(w_conv.shape, BF16),
            pltpu.SemaphoreType.DMA((11,)),
        ],
        name="prepare",
    )(times, jnp.asarray(wave_tables()), w_out_t, w_in, gain, w1, w2t, w_conv)


def wide(col):
    return jnp.concatenate([col] * (PIX // 128), axis=1)


def chain_kernel(
    times, table, recv, w_fwd, w_bwd, emb, rows, cols, w_in,
    sent, lat, stat, act, slope, taps, total,
):
    section, index = position()
    rid = row_index((8, PIX))
    upper = rid < CH
    lane = lax.broadcasted_iota(jnp.int32, (8, 128), 1)
    column = lane % SIDE
    col_ok = {1: column > 0, 0: None, -1: column < SIDE - 1}
    low_ok, high_ok = lane >= SIDE, lane < 128 - SIDE
    srow = row_index((8, C))
    supper = srow < CH
    in8 = doubled(w_in[...])
    in5 = jnp.where(supper, in8, 0.0)
    half_gain = rows[80:81]

    def piece(x, v):
        return x[:, 128 * v : 128 * v + 128]

    def moved(x, d):
        return x if d == 0 else jnp.where(col_ok[d], rolled(x, d, 1), 0.0)

    def moved_low(x, d):
        y = rolled(x, SIDE + d, 1)
        return jnp.where(low_ok if d == 0 else low_ok & col_ok[d], y, 0.0)

    def moved_high(x, d):
        y = rolled(x, d - SIDE, 1)
        return jnp.where(high_ok if d == 0 else high_ok & col_ok[d], y, 0.0)

    got = [recv[i] for i in range(16)]

    def gathered(base):
        parts = []
        for v in range(8):
            at = base + SIDE * (v % 2)
            parts.extend(got[(8 * q + v) // 2][:, at : at + SIDE] for q in range(4))
        return doubled(jnp.concatenate(parts, axis=1))

    latent0, target8 = gathered(0), gathered(2 * SIDE)

    def coefs(s):
        now = times[s]
        last = s == STEPS - 1
        after = times[jnp.minimum(s + 1, STEPS - 1)]
        root = jnp.where(last, 1.0, table[0, after])
        rest = jnp.where(last, 0.0, table[2, after])
        keep = root * table[1, now]
        return keep, rest - keep * table[2, now]

    def forward(s, l8):
        keep, nc = coefs(s)
        lat[s] = l8
        r1, r2, r3 = rolled(l8, -1, 0), rolled(l8, -2, 0), rolled(l8, -3, 0)
        x0 = jnp.where(upper, l8, l8 * l8)
        x1 = l8 * jnp.where(upper, r1, r2)
        m0 = jnp.sum(x0, axis=1, keepdims=True)
        m1 = jnp.sum(x1, axis=1, keepdims=True)
        p0 = rows[0:8] * m0
        p1 = rows[8:16] * m1
        avg = jnp.sum(jnp.where(supper, p0, 0.0), axis=0, keepdims=True)
        sq = jnp.sum(jnp.where(supper, 0.0, p0) + p1, axis=0, keepdims=True)
        rstd = lax.rsqrt(sq - avg * avg + EPS)
        scale = rstd * half_gain
        stat[s, 0:1] = avg
        stat[s, 1:2] = rstd
        stat[s, 2:3] = scale
        wz = jnp.where(srow == CH, -avg * scale, in5 * scale)
        a = wz.astype(BF16).astype(F32)
        wzs = jnp.concatenate([a, a, wz - a], axis=0).T.astype(BF16)
        hom = jnp.where(upper, l8, jnp.where(rid == CH, 1.0, 0.0))
        d = hom.astype(BF16).astype(F32)
        ls = jnp.concatenate([d, hom - d, d], axis=0).astype(BF16)
        linear = (
            wide(cols[0]) * l8 + wide(cols[1]) * r1 + wide(cols[2]) * r2 + wide(cols[3]) * r3
        )
        linear = keep * l8 + nc * (linear + wide(emb[s]))
        tiles = [slice(j * TILE, (j + 1) * TILE) for j in range(PIX // TILE)]
        hs = [dot(wzs, ls[:, at]) for at in tiles]
        for at, h in zip(tiles, hs):
            t = jnp.tanh(h)
            u = h * t
            narrow = (h + u).astype(BF16)
            act[s, :, at] = narrow
            taps[:, at] = dot(w_fwd[...], narrow)
            slope[s, :, at] = ((1.0 + t) + (h - u * t)).astype(BF16)

        def tap(dy, dx, v):
            k = 8 * (3 * dy + dx)
            return taps[k : k + 8, 128 * v : 128 * v + 128]

        out = []
        for v in range(8):
            conv = None
            for dx in (1, 0, 2):
                d = 1 - dx
                part = tap(1, dx, v)
                if v > 0:
                    part = part + tap(0, dx, v - 1)
                if v < 7:
                    part = part + tap(2, dx, v + 1)
                part = moved(part, d)
                conv = part if conv is None else conv + part
                if v == 0:
                    conv = conv + moved_low(tap(0, dx, 7), d)
                if v == 7:
                    conv = conv + moved_high(tap(2, dx, 0), d)
            conv = conv + rolled(conv, 4, 0)
            out.append(piece(linear, v) + nc * conv)
        return jnp.concatenate(out, axis=1)

    final = lax.fori_loop(0, STEPS, forward, latent0)
    lat[STEPS] = final
    total[...] = jnp.zeros_like(total)
    erow = row_index((16, C)) < CH

    def backward(i, adj):
        s = STEPS - 1 - i
        keep, nc = coefs(s)
        l8 = lat[s]
        avg, rstd, scale = stat[s, 0:1], stat[s, 1:2], stat[s, 2:3]
        ng = nc * adj
        head = ng.astype(BF16).astype(F32)
        x = jnp.where(upper, head, ng - head)
        first, last = piece(x, 0), piece(x, 7)
        above, same, below = [], [], []
        for d in (-1, 0, 1):
            ys = [moved(piece(x, v), d) for v in range(8)]
            same.append(jnp.concatenate(ys, axis=1))
            above.append(jnp.concatenate(ys[1:] + [moved_high(first, d)], axis=1))
            below.append(jnp.concatenate([moved_low(last, d)] + ys[:7], axis=1))
        pad = jnp.zeros_like(x)
        a80 = jnp.concatenate(above + same + below + [pad], axis=0).astype(BF16)
        col = jnp.concatenate([a80, a80], axis=0)
        ws = in8 * scale
        whead = ws.astype(BF16).astype(F32)
        wd = jnp.where(supper, whead, ws - whead)
        q = (-0.5 * rstd * rstd * rstd) * half_gain
        qa = q * avg
        per = jnp.where(erow, -2.0 * qa, q)
        one = jnp.where(erow, 2.0 * qa * avg - scale, -qa)
        phi = [rows[16 * (c + 1) : 16 * (c + 2)] * per for c in range(CH)]
        phi = jnp.concatenate(phi + [rows[0:16] * one, wd, jnp.zeros_like(wd)], axis=0).astype(BF16)
        tiles = [slice(j * TILE, (j + 1) * TILE) for j in range(PIX // TILE)]
        gs = [dot(w_bwd[...], col[:, at]) for at in tiles]
        outs = []
        for at, g in zip(tiles, gs):
            outs.append(dot(phi, g.astype(BF16) * slope[s, :, at]))
        total[...] += dot(act[s], a80, NT)
        z = jnp.concatenate(outs, axis=1)
        dl = z[80:88]
        dl = dl + rolled(dl, 4, 0)
        acc0, acc1 = z[64:72], z[72:80]
        for c in range(CH):
            lc = l8[c : c + 1]
            acc0 = acc0 + z[16 * c : 16 * c + 8] * lc
            acc1 = acc1 + z[16 * c + 8 : 16 * c + 16] * lc
        c0 = jnp.sum(acc0, axis=1, keepdims=True)
        c1 = jnp.sum(acc1, axis=1, keepdims=True)
        c0 = jnp.broadcast_to(c0, (8, 128))
        c1 = jnp.broadcast_to(c1, (8, 128))
        up8 = upper[:, :128]
        c0r, c1r = rolled(c0, 4, 0), rolled(c1, 4, 0)
        dm = jnp.where(up8, c0, c0r)
        d0 = 2.0 * jnp.where(up8, c0r, c0)
        d1 = jnp.where(up8, c1, c1r)
        d3 = rolled(d1, 1, 0)
        d2 = jnp.where(up8, c1r, c1)
        d2 = d2 + rolled(d2, 2, 0)
        r1, r2, r3 = rolled(l8, -1, 0), rolled(l8, -2, 0), rolled(l8, -3, 0)
        a1, a2, a3 = rolled(adj, -1, 0), rolled(adj, -2, 0), rolled(adj, -3, 0)
        linear = (
            wide(cols[4]) * adj + wide(cols[5]) * a1 + wide(cols[6]) * a2 + wide(cols[7]) * a3
        )
        linear = keep * adj + nc * linear + dl
        stats = wide(dm) + wide(d0) * l8 + wide(d1) * r1 + wide(d2) * r2 + wide(d3) * r3
        return linear + stats

    lax.fori_loop(0, STEPS, backward, final - target8)
    turned = total[...].T
    for k in range(9):
        part = turned[8 * k : 8 * k + 8]
        part = part + rolled(part, 4, 0)
        sent[4 * k : 4 * k + 4] = part[0:4]
    mine = lat[section + 1, :, pl.ds(pl.multiple_of(index % 4 // 2 * 512, 512), 512)]
    blank = jnp.zeros((4, C - 128), F32)
    for v in range(4):
        sent[36 + 4 * v : 40 + 4 * v] = jnp.concatenate([piece(mine, v)[0:4], blank], axis=1)


def chain(times, table, recv, w_fwd, w_bwd, emb, rows, cols, w_in):
    smem = pl.BlockSpec(memory_space=pltpu.SMEM)
    vmem = pl.BlockSpec(memory_space=pltpu.VMEM)
    return pl.pallas_call(
        chain_kernel,
        out_shape=jax.ShapeDtypeStruct((56, C), F32),
        in_specs=[smem] * 2 + [vmem] * 7,
        out_specs=vmem,
        scratch_shapes=[
            pltpu.VMEM((STEPS + 1, 8, PIX), F32),
            pltpu.VMEM((STEPS, 8, C), F32),
            pltpu.VMEM((STEPS, C, PIX), BF16),
            pltpu.VMEM((STEPS, C, PIX), BF16),
            pltpu.VMEM((80, PIX), F32),
            pltpu.VMEM((C, 80), F32),
        ],
        name="chain",
    )(times, table, recv, w_fwd, w_bwd, emb, rows, cols, w_in)


def finish_kernel(own, other, w_out_t, path, grad):
    index = position()[1]
    core, turn = index % 2, (128 - SIDE * (index // 4)) % 128
    for r in range(2):
        k = 36 + 4 * r
        mine = jnp.where(core == 0, own[k : k + 4, 0:128], own[k + 8 : k + 12, 0:128])
        theirs = jnp.where(core == 0, other[k : k + 4, 0:128], other[k + 8 : k + 12, 0:128])
        first = jnp.where(core == 0, mine, theirs)
        second = jnp.where(core == 0, theirs, mine)
        for m, x in enumerate((first, second)):
            x = pltpu.roll(x, turn, 1)
            for c in range(CH):
                path[0, m, c, r : r + 1] = x[c : c + 1, 0:SIDE]
    width = grad.shape[1]
    weights = jnp.concatenate([w_out_t[...], jnp.zeros((CH, 384 - C), F32)], axis=1)
    weights = pltpu.roll(weights, (384 - width * index) % 384, 1)[:, :128]
    w_head = weights.astype(BF16).astype(F32)
    left = jnp.concatenate([w_head, w_head, weights - w_head, weights * 0.0], axis=0)
    left = left.T[:24].astype(BF16)
    both = own[0:36] + other[0:36]
    head = both.astype(BF16).astype(F32)
    tail = both - head
    for k in range(9):
        at = slice(4 * k, 4 * k + 4)
        right = jnp.concatenate([head[at], tail[at], head[at], tail[at]], axis=0)
        grad[k] = dot(left, right.astype(BF16))[:width]


def finish(own, other, w_out_t, width):
    vmem = pl.BlockSpec(memory_space=pltpu.VMEM)
    return pl.pallas_call(
        finish_kernel,
        out_shape=(
            jax.ShapeDtypeStruct((1, 2, CH, 2, SIDE), F32),
            jax.ShapeDtypeStruct((9, width, C), F32),
        ),
        in_specs=[vmem] * 3,
        out_specs=(vmem, vmem),
        name="finish",
    )(own, other, w_out_t)


def local(noise, target, timesteps, w_in, gn_gain, w_time1, w_time2, w_conv, w_out):
    count = lax.axis_size("tensor")
    recv = lax.all_to_all(pack(noise, target), "tensor", 0, 0, tiled=True)
    w_out_t = w_out.T
    made = prepare(timesteps, w_out_t, w_in, gn_gain, w_time1, w_time2.T, w_conv)
    own = chain(timesteps, jnp.asarray(schedule_tables()), recv, *made, w_in)
    other = lax.ppermute(own, "tensor", [(i, i ^ 1) for i in range(count)])
    path, grad = finish(own, other, w_out_t, C // count)
    return path, jnp.swapaxes(grad, 1, 2)


def solution(mesh):
    placed = (
        P(None, None, "tensor", None),
        P(None, None, "tensor", None),
        P(),
        P(),
        P(),
        P(),
        P(),
        P(),
        P(),
    )
    return jax.shard_map(
        local,
        mesh=mesh,
        in_specs=placed,
        out_specs=(P("section", None, None, "tensor", None), P(None, None, "tensor")),
        check_vma=False,
    )
```

time: 81.5 us -> 50.1 us (0.61)
  Pallas kernels: 63.7 us -> 39.5 us
  local copies, waits for them, and re-layouts: 6.87 us -> 1.22 us
  other arithmetic: 2.86 us -> 0 us
  waiting for transfers between devices: 0.01 us -> 1.4 us
    pallas_call x1 -> x2, Pallas kernels: 54 us -> 31.3 us  [the longest x1 29.9 us: chain(): pl.pallas_call(chain_kernel, out_shape=jax.ShapeDtypeStruct((56, C), F32)...]
    reshape x2 -> x0, local copies, waits for them, and re-layouts: 1.56 us -> none  [the longest x1 0.78 us: local(): noise.reshape(2, CH, 2 * SIDE)]
    unnamed x5 -> x4, local copies, waits for them, and re-layouts: 2.72 us -> 1.22 us
    pallas_call x1, Pallas kernels: 7.6 us -> 6.18 us  [prepare(): pl.pallas_call(prepare_kernel, out_shape=(jax.ShapeDtypeStruct((80, C), B...]
    ppermute x1, waiting for transfers between devices: 0.01 us -> 1.39 us  [local(): other = lax.ppermute(own, 'tensor', [(i, i ^ 1) for i in range(count)])]
    broadcast_in_dim x1 -> x0, local copies, waits for them, and re-layouts: 1.24 us -> none  [local(): gn_gain[None]]
  transfers between devices with their start and end apart: 2 -> 2, of which waited for: 0 -> 1; matrix products, arithmetic and copies ran while one was open for 6% -> 0% of each run, Pallas kernels for 9% -> 12%
where the time goes in v2:
time: 50.1 us; the launch traced here: 49.8 us
  Pallas kernels  39.5 us (79%)
  starting transfers between devices  7 us (14%)
  waiting for transfers between devices  1.4 us (3%)
  local copies, waits for them, and re-layouts  1.22 us (2%)
  between operations  0.66 us (1%)
    pallas_call x1, Pallas kernels, chain(): pl.pallas_call(chain_kernel, out_shape=jax.ShapeDtypeStruct((56, C), F32)...  29.9 us
    all_to_all x1, starting transfers between devices, local(): recv = lax.all_to_all(pack(noise, target), 'tensor', 0, 0, tiled=True)  6.9 us
    pallas_call x1, Pallas kernels, prepare(): pl.pallas_call(prepare_kernel, out_shape=(jax.ShapeDtypeStruct((80, C), B...  6.18 us
    pallas_call x1, Pallas kernels, finish(): pl.pallas_call(finish_kernel, out_shape=(jax.ShapeDtypeStruct((1, 2, CH,...  2.01 us
    pallas_call x1, Pallas kernels, pack(): pl.pallas_call(pack_kernel, out_shape=jax.ShapeDtypeStruct((16, CH, 128),...  1.39 us
    ppermute x1, waiting for transfers between devices, local(): other = lax.ppermute(own, 'tensor', [(i, i ^ 1) for i in range(count)])  1.39 us
    unnamed x4, local copies, waits for them, and re-layouts  1.22 us
  transfers between devices with their start and end apart: 2, of which 1 were waited for; matrix products, arithmetic and copies ran while one was open for 0% of the time, Pallas kernels for 12%

profile of v2, /device:TPU:1, one launch (start us, length us, event | category | flops | bytes accessed | tf_op | source)
XLA Modules:
  0.0 49.8 jit_solution(2515803008558058036)
XLA Ops:
  0.6 1.4 %pack.1 = f32[16,4,128]{2,1,0:T(4,128)} custom-call(f32[2,4,2,32]{3,2,1,0:T(2,128)} %noise.1, f32[2,4,2,32]{3,2,1,0:T(2,128)} %target.1), custom_call_target="tpu_custom_call" | custom-call | tf_op jit(solution)/shard_map/pack/pallas_call | solution.py:93
  2.0 6.9 %all-to-all-start = ((f32[16,4,128]{2,1,0:T(4,128)}), f32[16,4,128]{2,1,0:T(4,128)S(1)}, u32[]{:S(2)}, u32[]{:S(2)}) async-start(f32[16,4,128]{2,1,0:T(4,128)} %pack.1), calls=%async_computation | async-start | bytes 65536 | tf_op jit(solution)/shard_map/all_to_all | solution.py:468
  8.9 6.2 %prepare.1 = (bf16[80,320]{1,0:T(8,128)(2,1)}, bf16[320,160]{1,0:T(8,128)(2,1)}, f32[16,8,128]{2,1,0:T(8,128)}, f32[88,320]{1,0:T(8,128)}, f32[8,8,128]{2,1,0:T(8,128)}) custom-call(s32[16]{0:T(128)} %times.3, f32[4,32,320]{2,1,0:T(8,128)} %constant.4.clone.waves, f32[4,320]{1,0:T(4,128)} %bitcast.4, f32[4,320]{1,0:T(4,128)} %w_in.3, f32[320]{0:T(512)} %gain.1, ...), custom_call_target="tpu_custom_call" | custom-call | tf_op jit(solution)/shard_map/prepare/pallas_call | solution.py:188
  15.1 0.0 all-to-all-done.recv
  15.1 0.0 copy-start
  15.1 0.6 %copy-done = f32[16,4,128]{2,1,0:T(4,128)} copy-done((f32[16,4,128]{2,1,0:T(4,128)}, f32[16,4,128]{2,1,0:T(4,128)S(1)}, u32[]{:S(2)}) %copy-start) | copy-done | bytes 32792
  15.7 29.9 %chain.1.own = f32[56,320]{1,0:T(8,128)} custom-call(s32[16]{0:T(128)} %times.3, f32[3,1024]{1,0:T(4,128)} %constant.5.clone.table, f32[16,4,128]{2,1,0:T(4,128)} %copy-done, bf16[80,320]{1,0:T(8,128)(2,1)} %get-tuple-element.9.w_fwd, bf16[320,160]{1,0:T(8,128)(2,1)} %get-tuple-element.10.w_bwd, f32[16,8,128]{2,1,0:T(8,128)} %get-tuple-element.11.emb, ...), custom_call_target="tpu_custom_call" | custom-call | tf_op jit(solution)/shard_map/chain/pallas_call | solution.py:407
  45.7 0.1 collective-permute-start
  45.8 1.4 %collective-permute-done.other = f32[56,320]{1,0:T(8,128)S(1)} collective-permute-done((f32[56,320]{1,0:T(8,128)}, f32[56,320]{1,0:T(8,128)S(1)}, u32[]{:S(2)}, u32[]{:S(2)}) %collective-permute-start) | collective-permute-done | bytes 71712 | tf_op jit(solution)/shard_map/ppermute | solution.py:472
  47.1 0.0 copy-start.1
  47.2 0.6 %copy-done.1 = f32[56,320]{1,0:T(8,128)} copy-done((f32[56,320]{1,0:T(8,128)}, f32[56,320]{1,0:T(8,128)S(1)}, u32[]{:S(2)}) %copy-start.1) | copy-done | bytes 71704
  47.8 2.0 %finish.1 = (f32[1,2,4,2,32]{4,3,2,1,0:T(2,128)}, f32[9,20,320]{2,1,0:T(8,128)}) custom-call(f32[56,320]{1,0:T(8,128)} %chain.1.own, f32[56,320]{1,0:T(8,128)} %copy-done.1, f32[4,320]{1,0:T(4,128)} %bitcast.5), custom_call_target="tpu_custom_call" | custom-call | tf_op jit(solution)/shard_map/finish/pallas_call | solution.py:454
Async XLA Ops:
  2.0 13.1 %all-to-all-start = ((f32[16,4,128]{2,1,0:T(4,128)}), f32[16,4,128]{2,1,0:T(4,128)S(1)}, u32[]{:S(2)}, u32[]{:S(2)}) async-start(f32[16,4,128]{2,1,0:T(4,128)} %pack.1), calls=%async_computation | async-start | bytes 65536 | tf_op jit(solution)/shard_map/all_to_all | solution.py:468
  15.1 0.6 %copy-start = (f32[16,4,128]{2,1,0:T(4,128)}, f32[16,4,128]{2,1,0:T(4,128)S(1)}, u32[]{:S(2)}) copy-start(f32[16,4,128]{2,1,0:T(4,128)S(1)} %all-to-all-done.recv) | copy-start | bytes 98308
  45.7 1.5 %collective-permute-start = (f32[56,320]{1,0:T(8,128)}, f32[56,320]{1,0:T(8,128)S(1)}, u32[]{:S(2)}, u32[]{:S(2)}) collective-permute-start(f32[56,320]{1,0:T(8,128)} %chain.1.own), channel_id=1, source_target_pairs={{0,1},{1,0},{2,3},{3,2},{4,5},{5,4},{6,7},{7,6},{8,9},{9,8},{10,11... | collective-permute-start | bytes 215048 | tf_op jit(solution)/shard_map/ppermute | solution.py:472
  47.1 0.6 %copy-start.1 = (f32[56,320]{1,0:T(8,128)}, f32[56,320]{1,0:T(8,128)S(1)}, u32[]{:S(2)}) copy-start(f32[56,320]{1,0:T(8,128)S(1)} %collective-permute-done.other) | copy-start | bytes 215044

commit v3 on v2

--- a/solution.py
+++ b/solution.py
@@ -80,6 +80,10 @@
     ).astype(np.float32)
 
 
+def near(x):
+    return pltpu.with_memory_space_constraint(x, pltpu.VMEM)
+
+
 def pack_kernel(noise, target, packed):
     for m in range(2):
         parts = [x[m, :, r, :] for x in (noise, target) for r in range(2)]
@@ -92,13 +96,19 @@
     vmem = pl.BlockSpec(memory_space=pltpu.VMEM)
     return pl.pallas_call(
         pack_kernel,
-        out_shape=jax.ShapeDtypeStruct((16, CH, 128), F32),
+        out_shape=pltpu.VMEM((16, CH, 128), F32),
         in_specs=[vmem] * 2,
         out_specs=vmem,
         name="pack",
     )(noise, target)
 
 
+def regrouped(x, buffer):
+    buffer[...] = x
+    size = C // GROUPS
+    return jnp.concatenate([buffer[pl.ds(k, GROUPS, stride=size), :] for k in range(size)], axis=0)
+
+
 def two(x):
     head = x.astype(BF16)
     return head, (x - head.astype(F32)).astype(BF16)
@@ -109,14 +119,22 @@
 
 
 def prepare_kernel(
-    times, waves, w_out_t, w_in, gain, w1_hbm, w2t_hbm, conv_hbm,
-    w_fwd, w_bwd, emb, rows, cols, w1, w2t, conv, sems,
+    times, tables, waves, w_out_t, w_in, gain, w1_hbm, w2t_hbm, conv_hbm,
+    w_fwd, w_bwd, emb, rows, cols, spread, means, steps, w1, w2t, conv, buffer, sems,
 ):
     copies = [pltpu.make_async_copy(conv_hbm.at[k], conv.at[k], sems.at[k]) for k in range(9)]
     copies.append(pltpu.make_async_copy(w1_hbm, w1, sems.at[9]))
     copies.append(pltpu.make_async_copy(w2t_hbm, w2t, sems.at[10]))
     for c in copies:
         c.start()
+    for s in range(STEPS):
+        now = times[s]
+        last = s == STEPS - 1
+        root = 1.0 if last else tables[0, times[s + 1]]
+        rest = 0.0 if last else tables[2, times[s + 1]]
+        keep = root * tables[1, now]
+        steps[0, s] = keep
+        steps[1, s] = rest - keep * tables[2, now]
     out8 = doubled(w_out_t[...])
     in8 = doubled(w_in[...])
     first = row_index((8, C)) < CH
@@ -129,10 +147,23 @@
     p1, p2, p3 = [p.astype(F32) for p in split(both, 3)]
     sums = dot(jnp.concatenate([p1, p2, p3], axis=0).astype(BF16), member)
     sums = (sums[0:16] + sums[16:32] + sums[32:48]) * (1.0 / (PIX * (C // GROUPS)))
-    rows[0:16] = sums
+    half_gain = 0.5 * gain[...].reshape(1, C)
+    place8 = row_index((8, C))
+    folded = jnp.where(place8 < CH, in8, jnp.where(place8 == CH, 1.0, 0.0)) * half_gain
+    gain8 = jnp.broadcast_to(half_gain, (8, C))
+    table = jnp.concatenate(
+        [folded, folded, folded, in8, sums, gain8, jnp.zeros((72, C), F32)], axis=0
+    )
+    ordered = regrouped(table.T, buffer)
+    spread[...] = ordered
+    for j in range(16):
+        means[j] = jnp.broadcast_to(ordered[0:GROUPS, 32 + j : 33 + j], (GROUPS, 128))
+    turned = ordered.T
     for c in range(CH):
-        rows[16 * (c + 1) : 16 * (c + 2)] = sums * w_in[c : c + 1]
-    rows[80:88] = jnp.broadcast_to(0.5 * gain[...].reshape(1, C), (8, C))
+        rows[16 * (c + 1) : 16 * (c + 2)] = turned[32:48] * turned[24 + c : 25 + c]
+    rows[0:16] = turned[32:48]
+    rows[80:88] = turned[48:56]
+    rows[88:96] = turned[24:32]
     for j in range(CH):
         ahead = jnp.sum(out8 * rolled(in8, -j, 0), axis=1, keepdims=True)
         back = jnp.sum(rolled(out8, -j, 0) * in8, axis=1, keepdims=True)
@@ -149,7 +180,7 @@
         at = lane // 8 == k
         right = jnp.concatenate([jnp.where(at, r_head, 0.0), jnp.where(at, r_tail, 0.0)], axis=1)
         acc = acc + dot(conv[k], right.astype(BF16))
-    full = acc[:, :128] + acc[:, 128:]
+    full = regrouped(acc[:, :128] + acc[:, 128:], buffer)
     head = full.astype(BF16).astype(F32)
     tail = full - head
     w_bwd[...] = jnp.concatenate([head[:, :80], tail[:, :80]], axis=1).astype(BF16)
@@ -188,22 +219,26 @@
     return pl.pallas_call(
         prepare_kernel,
         out_shape=(
-            jax.ShapeDtypeStruct((80, C), BF16),
-            jax.ShapeDtypeStruct((C, 160), BF16),
-            jax.ShapeDtypeStruct((STEPS, 8, 128), F32),
-            jax.ShapeDtypeStruct((88, C), F32),
-            jax.ShapeDtypeStruct((8, 8, 128), F32),
+            pltpu.VMEM((80, C), BF16),
+            pltpu.VMEM((C, 160), BF16),
+            pltpu.VMEM((STEPS, 8, 128), F32),
+            pltpu.VMEM((96, C), F32),
+            pltpu.VMEM((8, 8, 128), F32),
+            pltpu.VMEM((C, 128), F32),
+            pltpu.VMEM((16, GROUPS, 128), F32),
+            pltpu.SMEM((2, STEPS), F32),
         ),
-        in_specs=[smem] + [vmem] * 4 + [hbm] * 3,
-        out_specs=(vmem,) * 5,
+        in_specs=[smem] * 2 + [vmem] * 4 + [hbm] * 3,
+        out_specs=(vmem,) * 7 + (smem,),
         scratch_shapes=[
             pltpu.VMEM(w1.shape, F32),
             pltpu.VMEM(w2t.shape, F32),
             pltpu.VMEM(w_conv.shape, BF16),
+            pltpu.VMEM((C, 128), F32),
             pltpu.SemaphoreType.DMA((11,)),
         ],
         name="prepare",
-    )(times, jnp.asarray(wave_tables()), w_out_t, w_in, gain, w1, w2t, w_conv)
+    )(times, jnp.asarray(schedule_tables()), jnp.asarray(wave_tables()), w_out_t, w_in, gain, w1, w2t, w_conv)
 
 
 def wide(col):
@@ -211,8 +246,8 @@
 
 
 def chain_kernel(
-    times, table, recv, w_fwd, w_bwd, emb, rows, cols, w_in,
-    sent, lat, stat, act, slope, taps, total,
+    recv, w_fwd, w_bwd, emb, rows, cols, spread, means, steps,
+    sent, lat, stat, act, half, slope, taps, total, ordered,
 ):
     section, index = position()
     rid = row_index((8, PIX))
@@ -221,10 +256,10 @@
     column = lane % SIDE
     col_ok = {1: column > 0, 0: None, -1: column < SIDE - 1}
     low_ok, high_ok = lane >= SIDE, lane < 128 - SIDE
-    srow = row_index((8, C))
-    supper = srow < CH
-    in8 = doubled(w_in[...])
-    in5 = jnp.where(supper, in8, 0.0)
+    supper = row_index((8, C)) < CH
+    glane = lax.broadcasted_iota(jnp.int32, (GROUPS, 128), 1)
+    slane = lax.broadcasted_iota(jnp.int32, (C, 128), 1)
+    in8 = rows[88:96]
     half_gain = rows[80:81]
 
     def piece(x, v):
@@ -253,13 +288,7 @@
     latent0, target8 = gathered(0), gathered(2 * SIDE)
 
     def coefs(s):
-        now = times[s]
-        last = s == STEPS - 1
-        after = times[jnp.minimum(s + 1, STEPS - 1)]
-        root = jnp.where(last, 1.0, table[0, after])
-        rest = jnp.where(last, 0.0, table[2, after])
-        keep = root * table[1, now]
-        return keep, rest - keep * table[2, now]
+        return steps[0, s], steps[1, s]
 
     def forward(s, l8):
         keep, nc = coefs(s)
@@ -278,9 +307,19 @@
         stat[s, 0:1] = avg
         stat[s, 1:2] = rstd
         stat[s, 2:3] = scale
-        wz = jnp.where(srow == CH, -avg * scale, in5 * scale)
+        k0, k1 = jnp.broadcast_to(m0, (8, 128)), jnp.broadcast_to(m1, (8, 128))
+        terms = [means[j] * k0[j : j + 1] for j in range(8)]
+        terms += [means[8 + j] * k1[j : j + 1] for j in range(8)]
+        gavg = (terms[0] + terms[1]) + (terms[2] + terms[3])
+        gsq = ((terms[4] + terms[5]) + (terms[6] + terms[7])) + (
+            ((terms[8] + terms[9]) + (terms[10] + terms[11]))
+            + ((terms[12] + terms[13]) + (terms[14] + terms[15]))
+        )
+        factor = lax.rsqrt(gsq - gavg * gavg + EPS)
+        factor = jnp.where(glane % 8 == CH, -gavg * factor, factor)
+        wz = spread[...] * jnp.concatenate([factor] * (C // GROUPS), axis=0)
         a = wz.astype(BF16).astype(F32)
-        wzs = jnp.concatenate([a, a, wz - a], axis=0).T.astype(BF16)
+        wzs = jnp.where(slane >= 16, wz - a, a).astype(BF16)[:, :24]
         hom = jnp.where(upper, l8, jnp.where(rid == CH, 1.0, 0.0))
         d = hom.astype(BF16).astype(F32)
         ls = jnp.concatenate([d, hom - d, d], axis=0).astype(BF16)
@@ -296,7 +335,7 @@
             narrow = (h + u).astype(BF16)
             act[s, :, at] = narrow
             taps[:, at] = dot(w_fwd[...], narrow)
-            slope[s, :, at] = ((1.0 + t) + (h - u * t)).astype(BF16)
+            half[s, :, at] = t.astype(BF16)
 
         def tap(dy, dx, v):
             k = 8 * (3 * dy + dx)
@@ -355,11 +394,16 @@
         phi = [rows[16 * (c + 1) : 16 * (c + 2)] * per for c in range(CH)]
         phi = jnp.concatenate(phi + [rows[0:16] * one, wd, jnp.zeros_like(wd)], axis=0).astype(BF16)
         tiles = [slice(j * TILE, (j + 1) * TILE) for j in range(PIX // TILE)]
+        for at in tiles:
+            t = half[s, :, at]
+            slope[:, at] = (1 + t) + act[s, :, at] * (1 - t)
         gs = [dot(w_bwd[...], col[:, at]) for at in tiles]
+        mid = PIX // 2
+        total[...] += dot(act[s, :, :mid], a80[:, :mid], NT)
         outs = []
         for at, g in zip(tiles, gs):
-            outs.append(dot(phi, g.astype(BF16) * slope[s, :, at]))
-        total[...] += dot(act[s], a80, NT)
+            outs.append(dot(phi, g.astype(BF16) * slope[:, at]))
+        total[...] += dot(act[s, :, mid:], a80[:, mid:], NT)
         z = jnp.concatenate(outs, axis=1)
         dl = z[80:88]
         dl = dl + rolled(dl, 4, 0)
@@ -390,7 +434,10 @@
         return linear + stats
 
     lax.fori_loop(0, STEPS, backward, final - target8)
-    turned = total[...].T
+    size = C // GROUPS
+    for k in range(size):
+        ordered[pl.ds(k, GROUPS, stride=size), 0:80] = total[GROUPS * k : GROUPS * k + GROUPS]
+    turned = ordered[:, 0:80].T
     for k in range(9):
         part = turned[8 * k : 8 * k + 8]
         part = part + rolled(part, 4, 0)
@@ -401,24 +448,26 @@
         sent[36 + 4 * v : 40 + 4 * v] = jnp.concatenate([piece(mine, v)[0:4], blank], axis=1)
 
 
-def chain(times, table, recv, w_fwd, w_bwd, emb, rows, cols, w_in):
+def chain(recv, w_fwd, w_bwd, emb, rows, cols, spread, means, steps):
     smem = pl.BlockSpec(memory_space=pltpu.SMEM)
     vmem = pl.BlockSpec(memory_space=pltpu.VMEM)
     return pl.pallas_call(
         chain_kernel,
-        out_shape=jax.ShapeDtypeStruct((56, C), F32),
-        in_specs=[smem] * 2 + [vmem] * 7,
+        out_shape=pltpu.VMEM((56, C), F32),
+        in_specs=[vmem] * 8 + [smem],
         out_specs=vmem,
         scratch_shapes=[
             pltpu.VMEM((STEPS + 1, 8, PIX), F32),
             pltpu.VMEM((STEPS, 8, C), F32),
             pltpu.VMEM((STEPS, C, PIX), BF16),
             pltpu.VMEM((STEPS, C, PIX), BF16),
+            pltpu.VMEM((C, PIX), BF16),
             pltpu.VMEM((80, PIX), F32),
             pltpu.VMEM((C, 80), F32),
+            pltpu.VMEM((C, 128), F32),
         ],
         name="chain",
-    )(times, table, recv, w_fwd, w_bwd, emb, rows, cols, w_in)
+    )(*[near(x) for x in (recv, w_fwd, w_bwd, emb, rows, cols, spread, means)], steps)
 
 
 def finish_kernel(own, other, w_out_t, path, grad):
@@ -468,9 +517,9 @@
     recv = lax.all_to_all(pack(noise, target), "tensor", 0, 0, tiled=True)
     w_out_t = w_out.T
     made = prepare(timesteps, w_out_t, w_in, gn_gain, w_time1, w_time2.T, w_conv)
-    own = chain(timesteps, jnp.asarray(schedule_tables()), recv, *made, w_in)
+    own = chain(recv, *made)
     other = lax.ppermute(own, "tensor", [(i, i ^ 1) for i in range(count)])
-    path, grad = finish(own, other, w_out_t, C // count)
+    path, grad = finish(near(own), near(other), near(w_out_t), C // count)
     return path, jnp.swapaxes(grad, 1, 2)
 
 

time: 50.1 us -> 41.8 us (0.83)
  Pallas kernels: 39.5 us -> 32.6 us
  local copies, waits for them, and re-layouts: 1.22 us -> 0.01 us
    pallas_call x3, Pallas kernels: 37.5 us -> 31.5 us  [the longest x1 24.3 us: chain(): pl.pallas_call(chain_kernel, out_shape=pltpu.VMEM((56, C), F32), in_specs...]
    unnamed x4 -> x2, local copies, waits for them, and re-layouts: 1.22 us -> 0.01 us
    pallas_call x1, Pallas kernels: 2.01 us -> 1.08 us  [finish(): pl.pallas_call(finish_kernel, out_shape=(jax.ShapeDtypeStruct((1, 2, CH,...]
  transfers between devices with their start and end apart: 2 -> 2, of which waited for: 1 -> 1; matrix products, arithmetic and copies ran while one was open for 0% -> 0% of each run, Pallas kernels for 12% -> 14%
where the time goes in v3:
time: 41.8 us; the launch traced here: 41.5 us
  Pallas kernels  32.6 us (78%)
  starting transfers between devices  7.36 us (18%)
  waiting for transfers between devices  0.93 us (2%)
  between operations  0.66 us (2%)
    pallas_call x1, Pallas kernels, chain(): pl.pallas_call(chain_kernel, out_shape=pltpu.VMEM((56, C), F32), in_specs...  24.3 us
    all_to_all x1, starting transfers between devices, local(): recv = lax.all_to_all(pack(noise, target), 'tensor', 0, 0, tiled=True)  6.9 us
    pallas_call x1, Pallas kernels, prepare(): pl.pallas_call(prepare_kernel, out_shape=(pltpu.VMEM((80, C), BF16), pltp...  5.8 us
    pallas_call x1, Pallas kernels, pack(): pl.pallas_call(pack_kernel, out_shape=pltpu.VMEM((16, CH, 128), F32), in_...  1.41 us
    pallas_call x1, Pallas kernels, finish(): pl.pallas_call(finish_kernel, out_shape=(jax.ShapeDtypeStruct((1, 2, CH,...  1.08 us
    ppermute x1, waiting for transfers between devices, local(): other = lax.ppermute(own, 'tensor', [(i, i ^ 1) for i in range(count)])  0.93 us
  transfers between devices with their start and end apart: 2, of which 1 were waited for; matrix products, arithmetic and copies ran while one was open for 0% of the time, Pallas kernels for 14%

profile of v3, /device:TPU:1, one launch (start us, length us, event | category | flops | bytes accessed | tf_op | source)
XLA Modules:
  0.0 41.5 jit_solution(8986078416664328729)
XLA Ops:
  0.6 1.4 %pack.1 = f32[16,4,128]{2,1,0:T(4,128)} custom-call(f32[2,4,2,32]{3,2,1,0:T(2,128)} %noise.1, f32[2,4,2,32]{3,2,1,0:T(2,128)} %target.1), custom_call_target="tpu_custom_call" | custom-call | tf_op jit(solution)/shard_map/pack/pallas_call | solution.py:97
  2.0 6.9 %all-to-all-start = ((f32[16,4,128]{2,1,0:T(4,128)}), f32[16,4,128]{2,1,0:T(4,128)S(1)}, u32[]{:S(2)}, u32[]{:S(2)}) async-start(f32[16,4,128]{2,1,0:T(4,128)} %pack.1), calls=%async_computation | async-start | bytes 65536 | tf_op jit(solution)/shard_map/all_to_all | solution.py:517
  8.9 0.0 copy-start
  8.9 5.8 %prepare.1 = (bf16[80,320]{1,0:T(8,128)(2,1)S(1)}, bf16[320,160]{1,0:T(8,128)(2,1)S(1)}, f32[16,8,128]{2,1,0:T(8,128)S(1)}, f32[96,320]{1,0:T(8,128)S(1)}, f32[8...) custom-call(s32[16]{0:T(128)} %times.1, ...), custom_call_target="tpu_custom_call" | custom-call | tf_op jit(solution)/shard_map/prepare/pallas_call | solution.py:219
  14.8 0.0 all-to-all-done.recv
  14.8 24.3 %chain.1.own = f32[56,320]{1,0:T(8,128)S(1)} custom-call(f32[16,4,128]{2,1,0:T(4,128)S(1)} %all-to-all-done.recv, bf16[80,320]{1,0:T(8,128)(2,1)S(1)} %get-tuple-element.12.w_fwd, bf16[320,160]{1,0:T(8,128)(2,1)S(1)} %get-tuple-element.13.w_bwd, f32[16,8,128]{2,1,0:T(8,128)S(1)} %get-tuple-element.14.emb, f32[96,320]{1,0:T(8,128)S(1)} %get-tuple-element.15.rows, ...), custom_call_target="tpu_custom_call" | custom-call | tf_op jit(solution)/shard_map/chain/pallas_call | solution.py:454
  39.0 0.5 %collective-permute-start = (f32[56,320]{1,0:T(8,128)S(1)}, f32[56,320]{1,0:T(8,128)S(1)}, u32[]{:S(2)}, u32[]{:S(2)}) collective-permute-start(f32[56,320]{1,0:T(8,128)S(1)} %chain.1.own), channel_id=1, source_target_pairs={{0,1},{1,0},{2,3},{3,2},{4,5},{5,4},{6,7},{7,6},{8,9},{9,8},{10,11... | collective-permute-start | bytes 215048 | tf_op jit(solution)/shard_map/ppermute | solution.py:521
  39.5 0.9 %collective-permute-done.other = f32[56,320]{1,0:T(8,128)S(1)} collective-permute-done((f32[56,320]{1,0:T(8,128)S(1)}, f32[56,320]{1,0:T(8,128)S(1)}, u32[]{:S(2)}, u32[]{:S(2)}) %collective-permute-start) | collective-permute-done | bytes 71712 | tf_op jit(solution)/shard_map/ppermute | solution.py:521
  40.4 0.0 copy-done
  40.4 1.1 %finish.1 = (f32[1,2,4,2,32]{4,3,2,1,0:T(2,128)}, f32[9,20,320]{2,1,0:T(8,128)}) custom-call(f32[56,320]{1,0:T(8,128)S(1)} %chain.1.own, f32[56,320]{1,0:T(8,128)S(1)} %collective-permute-done.other, f32[4,320]{1,0:T(4,128)S(1)} %bitcast.4), custom_call_target="tpu_custom_call" | custom-call | tf_op jit(solution)/shard_map/finish/pallas_call | solution.py:503
Async XLA Ops:
  2.0 12.7 %all-to-all-start = ((f32[16,4,128]{2,1,0:T(4,128)}), f32[16,4,128]{2,1,0:T(4,128)S(1)}, u32[]{:S(2)}, u32[]{:S(2)}) async-start(f32[16,4,128]{2,1,0:T(4,128)} %pack.1), calls=%async_computation | async-start | bytes 65536 | tf_op jit(solution)/shard_map/all_to_all | solution.py:517
  8.9 31.5 %copy-start = (f32[320,4]{0,1:T(4,128)S(1)}, f32[320,4]{0,1:T(4,128)}, u32[]{:S(2)}) copy-start(f32[320,4]{0,1:T(4,128)} %param.19) | copy-start | bytes 15364
  39.0 1.4 %collective-permute-start = (f32[56,320]{1,0:T(8,128)S(1)}, f32[56,320]{1,0:T(8,128)S(1)}, u32[]{:S(2)}, u32[]{:S(2)}) collective-permute-start(f32[56,320]{1,0:T(8,128)S(1)} %chain.1.own), channel_id=1, source_target_pairs={{0,1},{1,0},{2,3},{3,2},{4,5},{5,4},{6,7},{7,6},{8,9},{9,8},{10,11... | collective-permute-start | bytes 215048 | tf_op jit(solution)/shard_map/ppermute | solution.py:521

commit v4 on v3

--- a/solution.py
+++ b/solution.py
@@ -196,11 +196,11 @@
     f_head, f_tail = two(jnp.concatenate(feats, axis=0))
     o_head, o_tail = two(out8)
     copies[9].wait()
+    copies[10].wait()
     w_head, w_tail = two(w1[...])
     z = dot(stacked(f_head, f_tail), w_head)
     z = 0.5 * (z[:STEPS] + z[STEPS:] + dot(f_head, w_tail))
     hidden = z + z * jnp.tanh(z)
-    copies[10].wait()
     w_head, w_tail = two(w2t[...])
     y = dot(stacked(o_head, o_tail), w_head)
     y = y[0:8] + y[8:16] + dot(o_head, w_tail)
@@ -239,6 +239,15 @@
         ],
         name="prepare",
     )(times, jnp.asarray(schedule_tables()), jnp.asarray(wave_tables()), w_out_t, w_in, gain, w1, w2t, w_conv)
+
+
+def repeated(step, state, group):
+    def several(i, state):
+        for k in range(group):
+            state = step(group * i + k, state)
+        return state
+
+    return lax.fori_loop(0, STEPS // group, several, state)
 
 
 def wide(col):
@@ -361,7 +370,7 @@
             out.append(piece(linear, v) + nc * conv)
         return jnp.concatenate(out, axis=1)
 
-    final = lax.fori_loop(0, STEPS, forward, latent0)
+    final = repeated(forward, latent0, 2)
     lat[STEPS] = final
     total[...] = jnp.zeros_like(total)
     erow = row_index((16, C)) < CH
@@ -398,12 +407,10 @@
             t = half[s, :, at]
             slope[:, at] = (1 + t) + act[s, :, at] * (1 - t)
         gs = [dot(w_bwd[...], col[:, at]) for at in tiles]
-        mid = PIX // 2
-        total[...] += dot(act[s, :, :mid], a80[:, :mid], NT)
         outs = []
         for at, g in zip(tiles, gs):
             outs.append(dot(phi, g.astype(BF16) * slope[:, at]))
-        total[...] += dot(act[s, :, mid:], a80[:, mid:], NT)
+        total[...] += dot(act[s], a80, NT)
         z = jnp.concatenate(outs, axis=1)
         dl = z[80:88]
         dl = dl + rolled(dl, 4, 0)
@@ -433,7 +440,7 @@
         stats = wide(dm) + wide(d0) * l8 + wide(d1) * r1 + wide(d2) * r2 + wide(d3) * r3
         return linear + stats
 
-    lax.fori_loop(0, STEPS, backward, final - target8)
+    repeated(backward, final - target8, 4)
     size = C // GROUPS
     for k in range(size):
         ordered[pl.ds(k, GROUPS, stride=size), 0:80] = total[GROUPS * k : GROUPS * k + GROUPS]
@@ -514,7 +521,7 @@
 
 def local(noise, target, timesteps, w_in, gn_gain, w_time1, w_time2, w_conv, w_out):
     count = lax.axis_size("tensor")
-    recv = lax.all_to_all(pack(noise, target), "tensor", 0, 0, tiled=True)
+    recv = lax.all_to_all(near(pack(noise, target)), "tensor", 0, 0, tiled=True)
     w_out_t = w_out.T
     made = prepare(timesteps, w_out_t, w_in, gn_gain, w_time1, w_time2.T, w_conv)
     own = chain(recv, *made)

time: 41.8 us -> 40.7 us (0.974)
  Pallas kernels: 32.6 us -> 31.3 us
    pallas_call x1, Pallas kernels: 24.3 us -> 23.2 us  [chain(): pl.pallas_call(chain_kernel, out_shape=pltpu.VMEM((56, C), F32), in_specs...]
  transfers between devices with their start and end apart: 2 -> 2, of which waited for: 1 -> 2; matrix products, arithmetic and copies ran while one was open for 0% -> 0% of each run, Pallas kernels for 14% -> 14%
where the time goes in v4:
time: 40.7 us; the launch traced here: 40.4 us
  Pallas kernels  31.3 us (77%)
  starting transfers between devices  7.39 us (18%)
  waiting for transfers between devices  1.04 us (3%)
  between operations  0.65 us (2%)
    pallas_call x1, Pallas kernels, chain(): pl.pallas_call(chain_kernel, out_shape=pltpu.VMEM((56, C), F32), in_specs...  23.2 us
    all_to_all x1, starting transfers between devices, local(): recv = lax.all_to_all(near(pack(noise, target)), 'tensor', 0, 0, tiled=True)  6.9 us
    pallas_call x1, Pallas kernels, prepare(): pl.pallas_call(prepare_kernel, out_shape=(pltpu.VMEM((80, C), BF16), pltp...  5.68 us
    pallas_call x1, Pallas kernels, pack(): pl.pallas_call(pack_kernel, out_shape=pltpu.VMEM((16, CH, 128), F32), in_...  1.41 us
    pallas_call x1, Pallas kernels, finish(): pl.pallas_call(finish_kernel, out_shape=(jax.ShapeDtypeStruct((1, 2, CH,...  1.08 us
    ppermute x1, waiting for transfers between devices, local(): other = lax.ppermute(own, 'tensor', [(i, i ^ 1) for i in range(count)])  0.93 us
  transfers between devices with their start and end apart: 2, of which 2 were waited for; matrix products, arithmetic and copies ran while one was open for 0% of the time, Pallas kernels for 14%

profile of v4, /device:TPU:1, one launch (start us, length us, event | category | flops | bytes accessed | tf_op | source)
XLA Modules:
  0.0 40.4 jit_solution(6157938337427522485)
XLA Ops:
  0.6 1.4 %pack.1 = f32[16,4,128]{2,1,0:T(4,128)} custom-call(f32[2,4,2,32]{3,2,1,0:T(2,128)} %noise.1, f32[2,4,2,32]{3,2,1,0:T(2,128)} %target.1), custom_call_target="tpu_custom_call" | custom-call | tf_op jit(solution)/shard_map/pack/pallas_call | solution.py:97
  2.0 6.9 %all-to-all-start = ((f32[16,4,128]{2,1,0:T(4,128)}), f32[16,4,128]{2,1,0:T(4,128)S(1)}, u32[]{:S(2)}, u32[]{:S(2)}) async-start(f32[16,4,128]{2,1,0:T(4,128)} %pack.1), calls=%async_computation | async-start | bytes 65536 | tf_op jit(solution)/shard_map/all_to_all | solution.py:524
  8.9 0.0 copy-start
  8.9 5.7 %prepare.1 = (bf16[80,320]{1,0:T(8,128)(2,1)S(1)}, bf16[320,160]{1,0:T(8,128)(2,1)S(1)}, f32[16,8,128]{2,1,0:T(8,128)S(1)}, f32[96,320]{1,0:T(8,128)S(1)}, f32[8...) custom-call(s32[16]{0:T(128)} %times.1, ...), custom_call_target="tpu_custom_call" | custom-call | tf_op jit(solution)/shard_map/prepare/pallas_call | solution.py:219
  14.6 0.1 all-to-all-done.recv
  14.7 23.2 %chain.1.own = f32[56,320]{1,0:T(8,128)S(1)} custom-call(f32[16,4,128]{2,1,0:T(4,128)S(1)} %all-to-all-done.recv, bf16[80,320]{1,0:T(8,128)(2,1)S(1)} %get-tuple-element.12.w_fwd, bf16[320,160]{1,0:T(8,128)(2,1)S(1)} %get-tuple-element.13.w_bwd, f32[16,8,128]{2,1,0:T(8,128)S(1)} %get-tuple-element.14.emb, f32[96,320]{1,0:T(8,128)S(1)} %get-tuple-element.15.rows, ...), custom_call_target="tpu_custom_call" | custom-call | tf_op jit(solution)/shard_map/chain/pallas_call | solution.py:461
  37.9 0.5 %collective-permute-start = (f32[56,320]{1,0:T(8,128)S(1)}, f32[56,320]{1,0:T(8,128)S(1)}, u32[]{:S(2)}, u32[]{:S(2)}) collective-permute-start(f32[56,320]{1,0:T(8,128)S(1)} %chain.1.own), channel_id=1, source_target_pairs={{0,1},{1,0},{2,3},{3,2},{4,5},{5,4},{6,7},{7,6},{8,9},{9,8},{10,11... | collective-permute-start | bytes 215048 | tf_op jit(solution)/shard_map/ppermute | solution.py:528
  38.4 0.9 %collective-permute-done.other = f32[56,320]{1,0:T(8,128)S(1)} collective-permute-done((f32[56,320]{1,0:T(8,128)S(1)}, f32[56,320]{1,0:T(8,128)S(1)}, u32[]{:S(2)}, u32[]{:S(2)}) %collective-permute-start) | collective-permute-done | bytes 71712 | tf_op jit(solution)/shard_map/ppermute | solution.py:528
  39.3 0.0 copy-done
  39.3 1.1 %finish.1 = (f32[1,2,4,2,32]{4,3,2,1,0:T(2,128)}, f32[9,20,320]{2,1,0:T(8,128)}) custom-call(f32[56,320]{1,0:T(8,128)S(1)} %chain.1.own, f32[56,320]{1,0:T(8,128)S(1)} %collective-permute-done.other, f32[4,320]{1,0:T(4,128)S(1)} %bitcast.4), custom_call_target="tpu_custom_call" | custom-call | tf_op jit(solution)/shard_map/finish/pallas_call | solution.py:510
Async XLA Ops:
  2.0 12.7 %all-to-all-start = ((f32[16,4,128]{2,1,0:T(4,128)}), f32[16,4,128]{2,1,0:T(4,128)S(1)}, u32[]{:S(2)}, u32[]{:S(2)}) async-start(f32[16,4,128]{2,1,0:T(4,128)} %pack.1), calls=%async_computation | async-start | bytes 65536 | tf_op jit(solution)/shard_map/all_to_all | solution.py:524
  8.9 30.4 %copy-start = (f32[320,4]{0,1:T(4,128)S(1)}, f32[320,4]{0,1:T(4,128)}, u32[]{:S(2)}) copy-start(f32[320,4]{0,1:T(4,128)} %param.19) | copy-start | bytes 15364
  37.9 1.4 %collective-permute-start = (f32[56,320]{1,0:T(8,128)S(1)}, f32[56,320]{1,0:T(8,128)S(1)}, u32[]{:S(2)}, u32[]{:S(2)}) collective-permute-start(f32[56,320]{1,0:T(8,128)S(1)} %chain.1.own), channel_id=1, source_target_pairs={{0,1},{1,0},{2,3},{3,2},{4,5},{5,4},{6,7},{7,6},{8,9},{9,8},{10,11... | collective-permute-start | bytes 215048 | tf_op jit(solution)/shard_map/ppermute | solution.py:528

commit v5 on v4

--- a/solution.py
+++ b/solution.py
@@ -370,7 +370,7 @@
             out.append(piece(linear, v) + nc * conv)
         return jnp.concatenate(out, axis=1)
 
-    final = repeated(forward, latent0, 2)
+    final = repeated(forward, latent0, 4)
     lat[STEPS] = final
     total[...] = jnp.zeros_like(total)
     erow = row_index((16, C)) < CH
@@ -440,7 +440,7 @@
         stats = wide(dm) + wide(d0) * l8 + wide(d1) * r1 + wide(d2) * r2 + wide(d3) * r3
         return linear + stats
 
-    repeated(backward, final - target8, 4)
+    repeated(backward, final - target8, 8)
     size = C // GROUPS
     for k in range(size):
         ordered[pl.ds(k, GROUPS, stride=size), 0:80] = total[GROUPS * k : GROUPS * k + GROUPS]

time: 40.7 us -> 40.4 us (level)
  no operation moved by 1% of the time
where the time goes in v5:
time: 40.4 us; the launch traced here: 40.2 us
  Pallas kernels  31.1 us (77%)
  starting transfers between devices  7.39 us (18%)
  waiting for transfers between devices  1.04 us (3%)
  between operations  0.65 us (2%)
    pallas_call x1, Pallas kernels, chain(): pl.pallas_call(chain_kernel, out_shape=pltpu.VMEM((56, C), F32), in_specs...  22.9 us
    all_to_all x1, starting transfers between devices, local(): recv = lax.all_to_all(near(pack(noise, target)), 'tensor', 0, 0, tiled=True)  6.9 us
    pallas_call x1, Pallas kernels, prepare(): pl.pallas_call(prepare_kernel, out_shape=(pltpu.VMEM((80, C), BF16), pltp...  5.68 us
    pallas_call x1, Pallas kernels, pack(): pl.pallas_call(pack_kernel, out_shape=pltpu.VMEM((16, CH, 128), F32), in_...  1.41 us
    pallas_call x1, Pallas kernels, finish(): pl.pallas_call(finish_kernel, out_shape=(jax.ShapeDtypeStruct((1, 2, CH,...  1.08 us
    ppermute x1, waiting for transfers between devices, local(): other = lax.ppermute(own, 'tensor', [(i, i ^ 1) for i in range(count)])  0.93 us
  transfers between devices with their start and end apart: 2, of which 2 were waited for; matrix products, arithmetic and copies ran while one was open for 0% of the time, Pallas kernels for 14%

profile of v5, /device:TPU:1, one launch (start us, length us, event | category | flops | bytes accessed | tf_op | source)
XLA Modules:
  0.0 40.2 jit_solution(7732326804487833918)
XLA Ops:
  0.6 1.4 %pack.1 = f32[16,4,128]{2,1,0:T(4,128)} custom-call(f32[2,4,2,32]{3,2,1,0:T(2,128)} %noise.1, f32[2,4,2,32]{3,2,1,0:T(2,128)} %target.1), custom_call_target="tpu_custom_call" | custom-call | tf_op jit(solution)/shard_map/pack/pallas_call | solution.py:97
  2.0 6.9 %all-to-all-start = ((f32[16,4,128]{2,1,0:T(4,128)}), f32[16,4,128]{2,1,0:T(4,128)S(1)}, u32[]{:S(2)}, u32[]{:S(2)}) async-start(f32[16,4,128]{2,1,0:T(4,128)} %pack.1), calls=%async_computation | async-start | bytes 65536 | tf_op jit(solution)/shard_map/all_to_all | solution.py:524
  8.9 0.0 copy-start
  8.9 5.7 %prepare.1 = (bf16[80,320]{1,0:T(8,128)(2,1)S(1)}, bf16[320,160]{1,0:T(8,128)(2,1)S(1)}, f32[16,8,128]{2,1,0:T(8,128)S(1)}, f32[96,320]{1,0:T(8,128)S(1)}, f32[8...) custom-call(s32[16]{0:T(128)} %times.1, ...), custom_call_target="tpu_custom_call" | custom-call | tf_op jit(solution)/shard_map/prepare/pallas_call | solution.py:219
  14.6 0.1 all-to-all-done.recv
  14.7 22.9 %chain.1.own = f32[56,320]{1,0:T(8,128)S(1)} custom-call(f32[16,4,128]{2,1,0:T(4,128)S(1)} %all-to-all-done.recv, bf16[80,320]{1,0:T(8,128)(2,1)S(1)} %get-tuple-element.12.w_fwd, bf16[320,160]{1,0:T(8,128)(2,1)S(1)} %get-tuple-element.13.w_bwd, f32[16,8,128]{2,1,0:T(8,128)S(1)} %get-tuple-element.14.emb, f32[96,320]{1,0:T(8,128)S(1)} %get-tuple-element.15.rows, ...), custom_call_target="tpu_custom_call" | custom-call | tf_op jit(solution)/shard_map/chain/pallas_call | solution.py:461
  37.7 0.5 %collective-permute-start = (f32[56,320]{1,0:T(8,128)S(1)}, f32[56,320]{1,0:T(8,128)S(1)}, u32[]{:S(2)}, u32[]{:S(2)}) collective-permute-start(f32[56,320]{1,0:T(8,128)S(1)} %chain.1.own), channel_id=1, source_target_pairs={{0,1},{1,0},{2,3},{3,2},{4,5},{5,4},{6,7},{7,6},{8,9},{9,8},{10,11... | collective-permute-start | bytes 215048 | tf_op jit(solution)/shard_map/ppermute | solution.py:528
  38.2 0.9 %collective-permute-done.other = f32[56,320]{1,0:T(8,128)S(1)} collective-permute-done((f32[56,320]{1,0:T(8,128)S(1)}, f32[56,320]{1,0:T(8,128)S(1)}, u32[]{:S(2)}, u32[]{:S(2)}) %collective-permute-start) | collective-permute-done | bytes 71712 | tf_op jit(solution)/shard_map/ppermute | solution.py:528
  39.1 0.0 copy-done
  39.1 1.1 %finish.1 = (f32[1,2,4,2,32]{4,3,2,1,0:T(2,128)}, f32[9,20,320]{2,1,0:T(8,128)}) custom-call(f32[56,320]{1,0:T(8,128)S(1)} %chain.1.own, f32[56,320]{1,0:T(8,128)S(1)} %collective-permute-done.other, f32[4,320]{1,0:T(4,128)S(1)} %bitcast.4), custom_call_target="tpu_custom_call" | custom-call | tf_op jit(solution)/shard_map/finish/pallas_call | solution.py:510
Async XLA Ops:
  2.0 12.7 %all-to-all-start = ((f32[16,4,128]{2,1,0:T(4,128)}), f32[16,4,128]{2,1,0:T(4,128)S(1)}, u32[]{:S(2)}, u32[]{:S(2)}) async-start(f32[16,4,128]{2,1,0:T(4,128)} %pack.1), calls=%async_computation | async-start | bytes 65536 | tf_op jit(solution)/shard_map/all_to_all | solution.py:524
  8.9 30.1 %copy-start = (f32[320,4]{0,1:T(4,128)S(1)}, f32[320,4]{0,1:T(4,128)}, u32[]{:S(2)}) copy-start(f32[320,4]{0,1:T(4,128)} %param.19) | copy-start | bytes 15364
  37.7 1.4 %collective-permute-start = (f32[56,320]{1,0:T(8,128)S(1)}, f32[56,320]{1,0:T(8,128)S(1)}, u32[]{:S(2)}, u32[]{:S(2)}) collective-permute-start(f32[56,320]{1,0:T(8,128)S(1)} %chain.1.own), channel_id=1, source_target_pairs={{0,1},{1,0},{2,3},{3,2},{4,5},{5,4},{6,7},{7,6},{8,9},{9,8},{10,11... | collective-permute-start | bytes 215048 | tf_op jit(solution)/shard_map/ppermute | solution.py:528
